TPU v7x, 256 devices: a whole 4x4x8 slice. The times are simulated.
256 devices in a mesh: district: 4 (over y_lo, core), sub: 64 (over x, y_hi, z).
Axes of the slice: x: 4, y: 4 (y_hi: 2, y_lo: 2; y = y_hi * 2 + y_lo), z: 8, core: 2. Of those that a mesh axis runs over, the one named last changes fastest.
Arguments:
- cost_terms: bfloat16 [8, 4096, 768], P('district', 'sub'), may hold values from -6 to 6
- neighbours: int32 [8, 4096, 4], P('district', 'sub'), may hold values from 0 to 4095, as said below
- relayout: int32 [8, 4096], P('district'), may hold values from 0 to 4095, as said below
- ownership: int32 [8, 4096], P('district', 'sub'), may hold values from 0 to 31
- capacity: float32 [16, 48], replicated, may hold values from -192 to 192
- coupling: bfloat16 [8, 768, 192], P('district'), may hold values from -0.21875 to 0.21875
- solve_factor: bfloat16 [8, 768, 768], P('district')
Outputs:
- control_plan: float32 [8, 4096, 768], P('district', 'sub')
- flow_prices: float32 [8, 4096, 192], P('district', 'sub')
- reservoir_duals: float32 [16, 48], replicated
Inputs may be any that keep to these rules, and one draw needn't show every extreme that they name: `neighbours`: each entry lies within 16 of its own balanced position and differs from it. `relayout`: each row is a permutation; of the subsystems at geographic positions s * 64 to (s + 1) * 64 - 1, exactly 1 go to balanced positions j * 64 to (j + 1) * 64 - 1, for every s and j. `ownership`: values of 16 or more mean that the subsystem draws from no reservoir.
All inputs are finite; a program needn't handle non-finite values.
Results may differ from a plain program's by a relative error of at most 0.018.
Values may be sent and summed in bfloat16 or wider, within the bound.
A program may use at most 64 MiB of HBM per device.

v0:
```python
import math

import jax
import jax.numpy as jnp
from jax import lax
from jax.experimental import pallas as pl
from jax.experimental.pallas import tpu as pltpu
from jax.sharding import PartitionSpec as P

MESH = pl.DeviceIdType.MESH
F32, BF16 = jnp.float32, jnp.bfloat16
HORIZON, UNKNOWNS, INTERFACE, BLOCK = 48, 768, 192, 64
RES, SUBS, DISTS = 16, 64, 4
REACH = 4
SLAB = 2 * REACH + 1
ROWS = 640
OWN = 32 + REACH * BLOCK
LANES = 256
STEP = 0.3
PEERS = SUBS - 1
OTHERS = 24


def dot(a, b):
    return jnp.dot(a, b, preferred_element_type=F32)


def dot_ta(a, b):
    return lax.dot_general(a, b, (((0,), (0,)), ((), ())), preferred_element_type=F32)


def dot_tb(a, b):
    return lax.dot_general(a, b, (((1,), (1,)), ((), ())), preferred_element_type=F32)


def iota(shape, dim):
    return lax.broadcasted_iota(jnp.int32, shape, dim)


def kernel(
    cost, coup, solve, own_ref, rt_ref, meta_ref, cap_ref,
    plan_o, price_o, dual_o,
    X, S, C, cs, cts, send1, recv1, send2, recv2, mbuf, offs, L2, lown, p4t, p5, mp, vfull,
    zf, zb, sacc, usum, ara, arb,
    load_sem, s1, r1, s2, r2, sm, rm, sa, ra, sb, rb,
):
    sub = lax.axis_index("sub")
    dist = lax.axis_index("district")
    sxy, sz = sub // 8, lax.rem(sub, 8)

    loads = []
    for d in range(2):
        loads.append(pltpu.make_async_copy(cost.at[d], X.at[d], load_sem.at[3 * d]))
        loads.append(pltpu.make_async_copy(solve.at[d], S.at[d], load_sem.at[3 * d + 1]))
        loads.append(pltpu.make_async_copy(coup.at[d], C.at[d], load_sem.at[3 * d + 2]))
    for copy in loads:
        copy.start()

    barrier = pltpu.get_barrier_semaphore()

    def hello(k, _):
        pl.semaphore_signal(
            barrier, inc=1, device_id={"sub": lax.rem(sub + k, SUBS)}, device_id_type=MESH
        )
        return 0

    lax.fori_loop(1, SUBS, hello, 0)

    def hello_other(k, _):
        there = lax.rem(dist + 1 + k // 8, DISTS)
        pl.semaphore_signal(
            barrier,
            inc=1,
            device_id={"district": there, "sub": lax.rem(k, 8) * 8 + sz},
            device_id_type=MESH,
        )
        return 0

    lax.fori_loop(0, OTHERS, hello_other, 0)

    first = []
    for d in range(2):
        for copy in loads[3 * d : 3 * d + 3]:
            copy.wait()
        cs_d = dot(X[d], S[d])
        cs[d * BLOCK : (d + 1) * BLOCK] = cs_d
        first.append(dot((-cs_d).astype(BF16), C[d]).astype(BF16))
    first = jnp.concatenate(first, axis=0)
    first = jnp.concatenate([first, jnp.zeros((2 * BLOCK, LANES - INTERFACE), BF16)], axis=1)
    lane = iota((2 * BLOCK, 2 * BLOCK), 1)
    row = iota((2 * BLOCK, 2 * BLOCK), 0)
    own_block = own_ref[...]
    to_dest = jnp.where(2 * own_block + lane // BLOCK == row, 1.0, 0.0).astype(BF16)
    eye = jnp.where(lane == row, 1.0, 0.0).astype(BF16)
    send1[0:REACH] = jnp.zeros((REACH, 2, LANES), BF16)
    send1[REACH + SUBS : SUBS + 2 * REACH] = jnp.zeros((REACH, 2, LANES), BF16)
    send1[REACH : REACH + SUBS] = dot(to_dest, first).astype(BF16).reshape(SUBS, 2, LANES)

    pl.semaphore_wait(barrier, PEERS + OTHERS)

    def meta_copy(k):
        return pltpu.make_async_remote_copy(
            src_ref=meta_ref,
            dst_ref=mbuf.at[2 * REACH - k],
            send_sem=sm,
            recv_sem=rm,
            device_id={"sub": lax.rem(sub + k - REACH + SUBS, SUBS)},
            device_id_type=MESH,
        )

    for k in range(SLAB):
        if k != REACH:
            meta_copy(k).start()

    def slab_copy(k):
        peer = lax.rem(sub + k, SUBS)
        return pltpu.make_async_remote_copy(
            src_ref=send1.at[pl.ds(peer, SLAB)],
            dst_ref=recv1.at[sub],
            send_sem=s1,
            recv_sem=r1,
            device_id={"sub": peer},
            device_id_type=MESH,
        )

    def send_slab(k, _):
        slab_copy(k).start()
        return 0

    lax.fori_loop(1, SUBS, send_slab, 0)
    recv1[sub] = send1[pl.ds(sub, SLAB)]
    mbuf[REACH] = meta_ref[...]

    p5[...] = dot_ta(to_dest, eye).astype(BF16)
    for d in range(2):
        cts_d = dot_ta(C[d], S[d]).astype(BF16)
        cts[d] = cts_d
        m_d = dot(cts_d, C[d])
        mp[d] = jnp.zeros((LANES, LANES), BF16)
        mp[d, 0:INTERFACE, 0:INTERFACE] = (-STEP * m_d).astype(BF16)
        ri = iota((LANES - INTERFACE, LANES - 128), 0)
        li = iota((LANES - INTERFACE, LANES - 128), 1)
        shift = jnp.where(li - (INTERFACE - 128) == ri + RES, 1.0, 0.0)
        mp[d, INTERFACE:LANES, 128:LANES] = shift.astype(BF16)

    rt = rt_ref[...]
    block_of, place_in = rt // BLOCK, lax.rem(rt, BLOCK)
    lane1 = iota((1, 2 * BLOCK), 1)

    def places(m):
        hit = block_of == sub + (m - REACH)
        place = jnp.sum(jnp.where(hit, place_in + 1, 0), axis=0, keepdims=True) - 1
        return jnp.where(place >= 0, place + BLOCK * lax.rem(lane1, 2), -1)

    def place_map(m):
        return jnp.where(places(m) == row, 1.0, 0.0).astype(BF16)

    p4t[...] = dot_ta(place_map(REACH), eye).astype(BF16)

    meta_all = pltpu.make_async_remote_copy(
        src_ref=mbuf.at[pl.ds(0, SLAB - 1)],
        dst_ref=mbuf.at[pl.ds(0, SLAB - 1)],
        send_sem=sm,
        recv_sem=rm,
        device_id={"sub": sub},
        device_id_type=MESH,
    )
    meta_all.wait_recv()
    eye64 = jnp.where(
        iota((BLOCK, 128), 0) == iota((BLOCK, 128), 1), 1.0, 0.0
    ).astype(BF16)
    zero32 = jnp.zeros((32, 16), F32)
    offs[0:32] = zero32
    offs[ROWS - 32 : ROWS] = zero32
    for m in range(SLAB):
        offs[32 + m * BLOCK : 32 + (m + 1) * BLOCK] = dot_tb(eye64, mbuf[m])
    diff = (iota((LANES, LANES), 1) - iota((LANES, LANES), 0)).astype(F32)
    for d in range(2):
        for i in range(3):
            cols = offs[192 * i : 192 * i + 256]
            near = jnp.where(diff == 0.0, 1.0, 0.0)
            for k in range(4):
                at = 4 * d + k
                near = near - jnp.where(diff == cols[:, at : at + 1], 0.25, 0.0)
            near = near.astype(BF16)
            L2[d, i] = dot(near, near)[32:224].astype(BF16)
        cols = offs[OWN : OWN + BLOCK]
        diff_own = (
            iota((BLOCK, 128), 1) - 32 - iota((BLOCK, 128), 0)
        ).astype(F32)
        near = jnp.where(diff_own == 0.0, 1.0, 0.0)
        for k in range(4):
            at = 4 * d + k
            near = near - jnp.where(diff_own == cols[:, at : at + 1], 0.25, 0.0)
        lown[d] = near.astype(BF16)

    for d in range(2):
        for top in (0, ROWS - 32):
            zf[d, top : top + 32] = jnp.zeros((32, LANES), F32)
            zb[d, top : top + 32] = jnp.zeros((32, LANES), BF16)
    slabs_all = pltpu.make_async_remote_copy(
        src_ref=recv1.at[pl.ds(0, PEERS)],
        dst_ref=recv1.at[pl.ds(0, PEERS)],
        send_sem=s1,
        recv_sem=r1,
        device_id={"sub": sub},
        device_id_type=MESH,
    )
    slabs_all.wait_recv()
    lane_e = iota((BLOCK, 128), 1) - (INTERFACE - 128)
    for m in range(SLAB):
        arrived = recv1[:, m].reshape(2 * BLOCK, LANES)
        rows_m = dot(place_map(m), arrived)
        top = 32 + m * BLOCK
        for d in range(2):
            part = rows_m[d * BLOCK : (d + 1) * BLOCK]
            owner = offs[top : top + BLOCK, 8 + d : 9 + d].astype(jnp.int32)
            mark = jnp.where((lane_e == owner) & (lane_e >= 0) & (lane_e < RES), 1.0, 0.0)
            low, high = part[:, 0:128], part[:, 128:LANES] + mark
            zf[d, top : top + BLOCK, 0:128] = low
            zf[d, top : top + BLOCK, 128:LANES] = high
            zb[d, top : top + BLOCK, 0:128] = low.astype(BF16)
            zb[d, top : top + BLOCK, 128:LANES] = high.astype(BF16)
    for d in range(2):
        sacc[d] = zf[d, OWN - 32 : OWN + 96]
        usum[d] = jnp.zeros((BLOCK, LANES), F32)

    def half(d, i):
        u = dot(L2[d, i], zb[d, 192 * i : 192 * i + 256])
        if i == 1:
            usum[d] += u[BLOCK : 2 * BLOCK]
        return u.astype(BF16)

    def advance(d, i, u):
        at = 32 + 192 * i
        z = zf[d, at : at + 192] + dot(u, mp[d])
        zf[d, at : at + 192] = z
        zb[d, at : at + 192] = z.astype(BF16)
        if i == 1:
            sacc[d] += z[32:160]

    def step(chunks):
        us = [(d, i, half(d, i)) for d in range(2) for i in chunks]
        for d, i, u in us:
            advance(d, i, u)

    def full_step(_, carry):
        step((0, 1, 2))
        return carry

    def marks(d):
        return zb[d, OWN : OWN + BLOCK, INTERFACE:LANES]

    def draw_part(flows):
        total = 0.0
        for d in range(2):
            first_marks = zb[d, OWN : OWN + BLOCK, INTERFACE : INTERFACE + RES]
            total = total + dot_ta(first_marks, flows[d])
        return total[:, 0:128]

    def folded(part):
        low, high = part[0:8, 0:64], part[8:16, 0:64]
        return jnp.concatenate([low, high], axis=1)

    def start_a(t):
        def go(k, _):
            z = lax.rem(sz + k, 8)
            pltpu.make_async_remote_copy(
                src_ref=ara.at[t, sz],
                dst_ref=ara.at[t, sz],
                send_sem=sa.at[t],
                recv_sem=ra.at[t],
                device_id={"sub": sxy * 8 + z},
                device_id_type=MESH,
            ).start()
            return 0

        lax.fori_loop(1, 8, go, 0)

    def start_b(t):
        here = dist * 8 + sxy

        def go(k, _):
            there = lax.rem(here + k, 32)
            pltpu.make_async_remote_copy(
                src_ref=arb.at[t, here],
                dst_ref=arb.at[t, here],
                send_sem=sb.at[t],
                recv_sem=rb.at[t],
                device_id={"district": there // 8, "sub": lax.rem(there, 8) * 8 + sz},
                device_id_type=MESH,
            ).start()
            return 0

        lax.fori_loop(1, 32, go, 0)

    def all_of(buf, t, count, send_sem, recv_sem):
        return pltpu.make_async_remote_copy(
            src_ref=buf.at[t, pl.ds(0, count)],
            dst_ref=buf.at[t, pl.ds(0, count)],
            send_sem=send_sem.at[t],
            recv_sem=recv_sem.at[t],
            device_id={"sub": sub},
            device_id_type=MESH,
        )

    def reduce_a(t, part):
        ara[t, sz] = folded(part)
        start_a(t)

    def reduce_b(t):
        all_of(ara, t, 7, sa, ra).wait_recv()
        arb[t, dist * 8 + sxy] = jnp.sum(ara[t], axis=0)
        start_b(t)

    def reduce_end(t):
        all_of(arb, t, 31, sb, rb).wait_recv()
        total = jnp.sum(arb[t], axis=0)
        return jnp.concatenate([total[:, 0:64], total[:, 64:128]], axis=0)

    def own_flows(d, top=OWN):
        return zb[d, top : top + BLOCK, 0:INTERFACE]

    lax.fori_loop(0, 3, full_step, 0)
    reduce_a(0, draw_part([own_flows(d) for d in range(2)]))
    lax.fori_loop(0, 2, full_step, 0)
    step((1,))

    us = [half(d, 1) for d in range(2)]
    back = []
    for d in range(2):
        prices = (STEP * usum[d]).astype(BF16)
        back.append(
            jnp.concatenate([prices[:, 0:INTERFACE], marks(d)], axis=1)
        )
    back = dot(p4t[...], jnp.concatenate(back, axis=0)).astype(BF16)
    send2[...] = back.reshape(SUBS, 2, LANES)

    def row_copy(k):
        peer = lax.rem(sub + k, SUBS)
        return pltpu.make_async_remote_copy(
            src_ref=send2.at[peer],
            dst_ref=recv2.at[sub],
            send_sem=s2,
            recv_sem=r2,
            device_id={"sub": peer},
            device_id_type=MESH,
        )

    def send_row(k, _):
        row_copy(k).start()
        return 0

    lax.fori_loop(1, SUBS, send_row, 0)
    recv2[sub] = send2[sub]

    stacks = [marks(d) for d in range(2)]
    near_marks = [
        dot(lown[d], zb[d, OWN - 32 : OWN + 96])[:, 128:LANES] for d in range(2)
    ]
    for d in range(2):
        advance(d, 1, us[d])
    price0 = []
    for d in range(2):
        sums = sacc[d][:, 0:INTERFACE]
        price0.append(dot(lown[d], sums.astype(BF16)))

    reduce_b(0)
    capacity = cap_ref[...]
    scale = 1.0 / math.sqrt(DISTS * 2 * SUBS * BLOCK / (2 * RES))
    duals = (reduce_end(0)[:, 0:HORIZON] - capacity) * scale
    wide = jnp.concatenate([duals, jnp.zeros((RES, INTERFACE - HORIZON), F32)], axis=1)

    binom = (1.0, 6.0, 15.0, 20.0)
    in_price = (1.0, -0.9, 0.27, -0.027)
    in_flow = (-1.0, 0.9, -0.27, 0.027)
    in_sum = (-4.0, 1.8, -0.36, 0.027)
    flows = []
    for d in range(2):
        powers = [wide]
        m_d = mp[d, 0:INTERFACE, 0:INTERFACE]
        for _ in range(4):
            powers.append(dot(powers[-1].astype(BF16), m_d) * (-1.0 / STEP))
        stack_price = [powers[j] * (in_price[j] / binom[j]) for j in range(4)]
        stack_flow = [powers[j + 1] * (in_flow[j] / binom[j]) for j in range(4)]
        stack_sum = [powers[j + 1] * (in_sum[j] / binom[j]) for j in range(4)]
        stack_price, stack_flow, stack_sum = [
            jnp.concatenate(t, axis=0).astype(BF16) for t in (stack_price, stack_flow, stack_sum)
        ]
        q8 = zf[d, OWN : OWN + BLOCK, 0:INTERFACE] + dot(stacks[d], stack_flow)
        flows.append(q8.astype(BF16))
        near_d = near_marks[d][:, INTERFACE - 128 : 128].astype(BF16)
        price_o[d] = STEP * (price0[d] + dot(near_d, stack_sum))
        vfull[d, 0:INTERFACE] = cts[d]
        vfull[d, INTERFACE:LANES] = dot(stack_price, cts[d]).astype(BF16)
    reduce_a(1, draw_part(flows))

    rows_all = pltpu.make_async_remote_copy(
        src_ref=recv2.at[pl.ds(0, PEERS)],
        dst_ref=recv2.at[pl.ds(0, PEERS)],
        send_sem=s2,
        recv_sem=r2,
        device_id={"sub": sub},
        device_id_type=MESH,
    )
    rows_all.wait_recv()
    mine = dot(p5[...], recv2[...].reshape(2 * BLOCK, LANES)).astype(BF16)
    for d in range(2):
        at = d * BLOCK
        plan_o[d] = -(cs[at : at + BLOCK] + dot(mine[at : at + BLOCK], vfull[d]))

    reduce_b(1)
    dual_o[...] = duals + (reduce_end(1)[:, 0:HORIZON] - capacity) * scale

    meta_all.wait_send()
    slabs_all.wait_send()
    rows_all.wait_send()
    for t in range(2):
        all_of(ara, t, 7, sa, ra).wait_send()
        all_of(arb, t, 31, sb, rb).wait_send()


def on_device(cost_terms, neighbours, relayout, ownership, capacity, coupling, solve_factor):
    sub = lax.axis_index("sub")
    mine = lax.dynamic_slice_in_dim(relayout, sub * BLOCK, BLOCK, axis=1)
    own = (mine // BLOCK).reshape(1, 2 * BLOCK)
    rt = relayout.reshape(2, SUBS, BLOCK).transpose(2, 1, 0).reshape(BLOCK, 2 * SUBS)
    places = sub * BLOCK + jnp.arange(BLOCK, dtype=jnp.int32)
    offsets = (neighbours - places[None, :, None]).transpose(0, 2, 1).reshape(8, BLOCK)
    meta = jnp.concatenate([offsets, ownership, jnp.zeros((6, BLOCK), jnp.int32)], axis=0)
    meta = jnp.pad(meta, ((0, 0), (0, 128 - BLOCK))).astype(BF16)
    vmem = pl.BlockSpec(memory_space=pltpu.VMEM)
    hbm = pl.BlockSpec(memory_space=pl.ANY)
    dma = pltpu.SemaphoreType.DMA
    return pl.pallas_call(
        kernel,
        out_shape=(
            jax.ShapeDtypeStruct((2, BLOCK, UNKNOWNS), F32),
            jax.ShapeDtypeStruct((2, BLOCK, INTERFACE), F32),
            jax.ShapeDtypeStruct((RES, HORIZON), F32),
        ),
        in_specs=[hbm, hbm, hbm, vmem, vmem, vmem, vmem],
        out_specs=(vmem, vmem, vmem),
        scratch_shapes=[
            pltpu.VMEM((2, BLOCK, UNKNOWNS), BF16),
            pltpu.VMEM((2, UNKNOWNS, UNKNOWNS), BF16),
            pltpu.VMEM((2, UNKNOWNS, INTERFACE), BF16),
            pltpu.VMEM((2 * BLOCK, UNKNOWNS), F32),
            pltpu.VMEM((2, INTERFACE, UNKNOWNS), BF16),
            pltpu.VMEM((SUBS + 2 * REACH, 2, LANES), BF16),
            pltpu.VMEM((SUBS, SLAB, 2, LANES), BF16),
            pltpu.VMEM((SUBS, 2, LANES), BF16),
            pltpu.VMEM((SUBS, 2, LANES), BF16),
            pltpu.VMEM((SLAB, 16, 128), BF16),
            pltpu.VMEM((ROWS, 16), F32),
            pltpu.VMEM((2, 3, 192, 256), BF16),
            pltpu.VMEM((2, BLOCK, 128), BF16),
            pltpu.VMEM((128, 128), BF16),
            pltpu.VMEM((128, 128), BF16),
            pltpu.VMEM((2, LANES, LANES), BF16),
            pltpu.VMEM((2, LANES, UNKNOWNS), BF16),
            pltpu.VMEM((2, ROWS, LANES), F32),
            pltpu.VMEM((2, ROWS, LANES), BF16),
            pltpu.VMEM((2, 128, LANES), F32),
            pltpu.VMEM((2, BLOCK, LANES), F32),
            pltpu.VMEM((2, 8, 8, 128), F32),
            pltpu.VMEM((2, 32, 8, 128), F32),
            dma((6,)),
            dma, dma, dma, dma, dma, dma,
            dma((2,)), dma((2,)), dma((2,)), dma((2,)),
        ],
        compiler_params=pltpu.CompilerParams(
            collective_id=0, has_side_effects=True, vmem_limit_bytes=48 * 1024 * 1024
        ),
    )(cost_terms, coupling, solve_factor, own, rt, meta, capacity)


def solution(mesh):
    placed = (
        P("district", "sub", None),
        P("district", "sub", None),
        P("district", None),
        P("district", "sub"),
        P(),
        P("district", None, None),
        P("district", None, None),
    )
    return jax.shard_map(
        on_device,
        mesh=mesh,
        in_specs=placed,
        out_specs=(P("district", "sub", None), P("district", "sub", None), P()),
        check_vma=False,
    )
```

profile of v0, /device:TPU:1, one launch (start us, length us, event | category | flops | bytes accessed | tf_op | source)
XLA Modules:
  0.0 65.1 jit_solution(5826226413191610889)
XLA Ops:
  0.6 0.7 %convert.13 = bf16[2,64]{1,0:T(2,128)(2,1)S(1)} convert(s32[2,64]{1,0:T(2,128)} %param.10) | non-fusion elementwise | flops 128 | bytes 768 | tf_op jit(solution)/shard_map/convert.3
  1.3 0.8 %and_select_fusion = s32[2,64]{1,0:T(2,128)S(1)} fusion(s32[2,4096]{1,0:T(2,128)} %param.9, s32[]{:T(128)S(6)} %select_n.8), kind=kLoop, calls=%fused_computation.2 | loop fusion | flops 1920 | bytes 1028 | tf_op jit(solution)/shard_map/jit(floor_divide)/jit(_where)/select_n | solution.py:426
  2.1 0.1 reshape.23.own_ref
  2.2 0.1 pad.8.clone
  2.3 0.7 %subtract_convert_fusion = bf16[2,64,4]{1,2,0:T(4,128)(2,1)S(1)} fusion(s32[2,64,4]{1,2,0:T(4,128)} %param.8, s32[64]{0:T(128)S(1)} %iota_add_fusion), kind=kLoop, calls=%fused_computation.1 | loop fusion | flops 1024 | bytes 3328 | tf_op jit(solution)/shard_map/convert.6
  2.9 0.1 maximum_maximum_fusion
  3.0 0.9 %reshape.24 = s32[2,64,64]{2,1,0:T(8,128)S(1)} reshape(s32[2,4096]{1,0:T(2,128)} %param.9) | data formatting | bytes 65536 | tf_op jit(solution)/shard_map/reshape | solution.py:427
  3.9 0.1 copy.12
  3.9 0.1 copy.14.rt_ref
  4.0 1.4 %copy.13.coup = bf16[2,768,192]{2,1,0:T(8,128)(2,1)S(1)} copy(bf16[2,768,192]{1,2,0:T(8,128)(2,1)} %param.12) | data formatting | bytes 1179648 | tf_op args[5]
  5.4 0.0 copy-start
  5.4 1.7 %copy-done = bf16[2,768,768]{2,1,0:T(8,128)(2,1)S(1)} copy-done((bf16[2,768,768]{2,1,0:T(8,128)(2,1)S(1)}, bf16[2,768,768]{2,1,0:T(8,128)(2,1)}, u32[]{:S(2)}) %copy-start) | copy-done | bytes 2359320
  7.0 0.0 copy-start.1
  7.0 0.9 %copy-done.1 = bf16[2,64,768]{2,1,0:T(8,128)(2,1)S(1)} copy-done((bf16[2,64,768]{2,1,0:T(8,128)(2,1)S(1)}, bf16[2,64,768]{2,1,0:T(8,128)(2,1)}, u32[]{:S(2)}) %copy-start.1) | copy-done | bytes 196632
  8.0 0.0 copy-start.2
  8.0 0.7 %copy-done.2 = f32[16,48]{1,0:T(8,128)S(1)} copy-done((f32[16,48]{1,0:T(8,128)S(1)}, f32[16,48]{1,0:T(8,128)}, u32[]{:S(2)}) %copy-start.2) | copy-done | bytes 3096
  8.7 54.4 %shard_map.94 = (f32[2,64,768]{2,1,0:T(8,128)S(1)}, f32[2,64,192]{2,1,0:T(8,128)S(1)}, f32[16,48]{1,0:T(8,128)S(1)}) custom-call(bf16[2,64,768]{2,1,0:T(8,128)(2,1)S(1)} %copy-done.1, bf16[2,768,192]{2,1,0:T(8,128)(2,1)S(1)} %copy.13.coup, bf16[2,768,768]{2,1,0:T(8,128)(2,1)S(1)} %copy-done, s32[1,128]{1,0:T(1,128)S(1)} %reshape.23.own_ref, ...), custom_call_target="tpu_custom_call" | custom-call | tf_op jit(solution)/shard_map/pallas_call | solution.py:435
  63.1 0.7 %copy.18 = f32[2,64,768]{2,1,0:T(8,128)} copy(f32[2,64,768]{2,1,0:T(8,128)S(1)} %get-tuple-element.6) | data formatting | bytes 786432
  63.9 0.7 %copy.19 = f32[2,64,192]{2,1,0:T(8,128)} copy(f32[2,64,192]{2,1,0:T(8,128)S(1)} %get-tuple-element.7) | data formatting | bytes 196608
  64.5 0.6 copy.20
  (3 shorter events, 0.0 us)
Async XLA Ops:
  5.4 1.7 %copy-start = (bf16[2,768,768]{2,1,0:T(8,128)(2,1)S(1)}, bf16[2,768,768]{2,1,0:T(8,128)(2,1)}, u32[]{:S(2)}) copy-start(bf16[2,768,768]{2,1,0:T(8,128)(2,1)} %solve.1) | copy-start | bytes 7077892
  7.0 0.9 %copy-start.1 = (bf16[2,64,768]{2,1,0:T(8,128)(2,1)S(1)}, bf16[2,64,768]{2,1,0:T(8,128)(2,1)}, u32[]{:S(2)}) copy-start(bf16[2,64,768]{2,1,0:T(8,128)(2,1)} %cost.1) | copy-start | bytes 589828
  8.0 0.7 %copy-start.2 = (f32[16,48]{1,0:T(8,128)S(1)}, f32[16,48]{1,0:T(8,128)}, u32[]{:S(2)}) copy-start(f32[16,48]{1,0:T(8,128)} %cap_ref.1) | copy-start | bytes 9220
where the time goes:
time: 65.5 us; the launch traced here: 65.1 us
  Pallas kernels  54.4 us (83%)
  local copies, waits for them, and re-layouts  7.79 us (12%)
  other arithmetic  2.21 us (3%)
  between operations  0.67 us (1%)
    pallas_call x1, Pallas kernels, on_device(): pl.pallas_call(kernel, out_shape=(jax.ShapeDtypeStruct((2, BLOCK, UNKNOWN...  54.4 us
    unnamed x10, local copies, waits for them, and re-layouts  6.64 us
    another operation x2, other arithmetic  1.38 us

commit v1 on v0

--- a/solution.py
+++ b/solution.py
@@ -19,6 +19,7 @@
 STEP = 0.3
 PEERS = SUBS - 1
 OTHERS = 24
+VMEM_LIMIT = 67043328 - 700 * 1024
 
 
 def dot(a, b):
@@ -38,9 +39,9 @@
 
 
 def kernel(
-    cost, coup, solve, own_ref, rt_ref, meta_ref, cap_ref,
+    cost, coup, solve, rel_h, near_h, owner_h, cap_h,
     plan_o, price_o, dual_o,
-    X, S, C, cs, cts, send1, recv1, send2, recv2, mbuf, offs, L2, lown, p4t, p5, mp, vfull,
+    X, S, C, cs, vfull, rel, near_in, owner_in, cap, meta, cts, send1, recv1, send2, recv2, mbuf, offs, L2, lown, p4t, p5, mp,
     zf, zb, sacc, usum, ara, arb,
     load_sem, s1, r1, s2, r2, sm, rm, sa, ra, sb, rb,
 ):
@@ -48,12 +49,18 @@
     dist = lax.axis_index("district")
     sxy, sz = sub // 8, lax.rem(sub, 8)
 
+    small = [
+        pltpu.make_async_copy(src, dst, load_sem.at[6 + i])
+        for i, (src, dst) in enumerate(
+            ((rel_h, rel), (near_h, near_in), (owner_h, owner_in), (cap_h, cap))
+        )
+    ]
     loads = []
     for d in range(2):
         loads.append(pltpu.make_async_copy(cost.at[d], X.at[d], load_sem.at[3 * d]))
         loads.append(pltpu.make_async_copy(solve.at[d], S.at[d], load_sem.at[3 * d + 1]))
         loads.append(pltpu.make_async_copy(coup.at[d], C.at[d], load_sem.at[3 * d + 2]))
-    for copy in loads:
+    for copy in small + loads:
         copy.start()
 
     barrier = pltpu.get_barrier_semaphore()
@@ -78,18 +85,28 @@
 
     lax.fori_loop(0, OTHERS, hello_other, 0)
 
+    for copy in small:
+        copy.wait()
+    place = iota((4, BLOCK), 1) + sub * BLOCK
+    told = [near_in[d] - place for d in range(2)] + [owner_in[...], jnp.zeros((6, BLOCK), jnp.int32)]
+    told = jnp.concatenate(told, axis=0).astype(F32)
+    meta[...] = jnp.concatenate([told, jnp.zeros((16, BLOCK), F32)], axis=1).astype(BF16)
+    mbuf[REACH] = meta[...]
+    here = rel[sub // 2]
+    here = jnp.where(lax.rem(sub, 2) == 0, here[:, 0:BLOCK], here[:, BLOCK:128]) // BLOCK
+    own_block = jnp.concatenate([here[0:1], here[1:2]], axis=1)
+
     first = []
     for d in range(2):
         for copy in loads[3 * d : 3 * d + 3]:
             copy.wait()
         cs_d = dot(X[d], S[d])
         cs[d * BLOCK : (d + 1) * BLOCK] = cs_d
-        first.append(dot((-cs_d).astype(BF16), C[d]).astype(BF16))
+        first.append(dot_tb((-cs_d).astype(BF16), C[d]).astype(BF16))
     first = jnp.concatenate(first, axis=0)
     first = jnp.concatenate([first, jnp.zeros((2 * BLOCK, LANES - INTERFACE), BF16)], axis=1)
     lane = iota((2 * BLOCK, 2 * BLOCK), 1)
     row = iota((2 * BLOCK, 2 * BLOCK), 0)
-    own_block = own_ref[...]
     to_dest = jnp.where(2 * own_block + lane // BLOCK == row, 1.0, 0.0).astype(BF16)
     eye = jnp.where(lane == row, 1.0, 0.0).astype(BF16)
     send1[0:REACH] = jnp.zeros((REACH, 2, LANES), BF16)
@@ -100,7 +117,7 @@
 
     def meta_copy(k):
         return pltpu.make_async_remote_copy(
-            src_ref=meta_ref,
+            src_ref=meta,
             dst_ref=mbuf.at[2 * REACH - k],
             send_sem=sm,
             recv_sem=rm,
@@ -112,11 +129,14 @@
         if k != REACH:
             meta_copy(k).start()
 
+    def slot_of(device):
+        return lax.rem(device, 2) * (SUBS // 2) + device // 2
+
     def slab_copy(k):
         peer = lax.rem(sub + k, SUBS)
         return pltpu.make_async_remote_copy(
             src_ref=send1.at[pl.ds(peer, SLAB)],
-            dst_ref=recv1.at[sub],
+            dst_ref=recv1.at[slot_of(sub)],
             send_sem=s1,
             recv_sem=r1,
             device_id={"sub": peer},
@@ -128,14 +148,13 @@
         return 0
 
     lax.fori_loop(1, SUBS, send_slab, 0)
-    recv1[sub] = send1[pl.ds(sub, SLAB)]
-    mbuf[REACH] = meta_ref[...]
+    recv1[slot_of(sub)] = send1[pl.ds(sub, SLAB)]
 
     p5[...] = dot_ta(to_dest, eye).astype(BF16)
     for d in range(2):
-        cts_d = dot_ta(C[d], S[d]).astype(BF16)
+        cts_d = dot(C[d], S[d]).astype(BF16)
         cts[d] = cts_d
-        m_d = dot(cts_d, C[d])
+        m_d = dot_tb(cts_d, C[d])
         mp[d] = jnp.zeros((LANES, LANES), BF16)
         mp[d, 0:INTERFACE, 0:INTERFACE] = (-STEP * m_d).astype(BF16)
         ri = iota((LANES - INTERFACE, LANES - 128), 0)
@@ -143,8 +162,14 @@
         shift = jnp.where(li - (INTERFACE - 128) == ri + RES, 1.0, 0.0)
         mp[d, INTERFACE:LANES, 128:LANES] = shift.astype(BF16)
 
-    rt = rt_ref[...]
-    block_of, place_in = rt // BLOCK, lax.rem(rt, BLOCK)
+    by_pair = rel[...].reshape(SUBS, 128)
+    eye_s = eye[0:SUBS, 0:SUBS]
+
+    def turned(values):
+        flat = dot_ta(values.astype(F32).astype(BF16), eye_s)
+        return jnp.concatenate([flat[0:BLOCK], flat[BLOCK:128]], axis=1).astype(jnp.int32)
+
+    block_of, place_in = turned(by_pair // BLOCK), turned(lax.rem(by_pair, BLOCK))
     lane1 = iota((1, 2 * BLOCK), 1)
 
     def places(m):
@@ -339,7 +364,7 @@
     def row_copy(k):
         peer = lax.rem(sub + k, SUBS)
         return pltpu.make_async_remote_copy(
-            src_ref=send2.at[peer],
+            src_ref=send2.at[slot_of(peer)],
             dst_ref=recv2.at[sub],
             send_sem=s2,
             recv_sem=r2,
@@ -352,7 +377,7 @@
         return 0
 
     lax.fori_loop(1, SUBS, send_row, 0)
-    recv2[sub] = send2[sub]
+    recv2[sub] = send2[slot_of(sub)]
 
     stacks = [marks(d) for d in range(2)]
     near_marks = [
@@ -366,7 +391,7 @@
         price0.append(dot(lown[d], sums.astype(BF16)))
 
     reduce_b(0)
-    capacity = cap_ref[...]
+    capacity = cap[...]
     scale = 1.0 / math.sqrt(DISTS * 2 * SUBS * BLOCK / (2 * RES))
     duals = (reduce_end(0)[:, 0:HORIZON] - capacity) * scale
     wide = jnp.concatenate([duals, jnp.zeros((RES, INTERFACE - HORIZON), F32)], axis=1)
@@ -420,32 +445,42 @@
         all_of(arb, t, 31, sb, rb).wait_send()
 
 
+def write_out(plan, price, dual, plan_o, price_o, dual_o, sems):
+    copies = [
+        pltpu.make_async_copy(src, dst, sems.at[i])
+        for i, (src, dst) in enumerate(((plan, plan_o), (price, price_o), (dual, dual_o)))
+    ]
+    for copy in copies:
+        copy.start()
+    for copy in copies:
+        copy.wait()
+
+
 def on_device(cost_terms, neighbours, relayout, ownership, capacity, coupling, solve_factor):
-    sub = lax.axis_index("sub")
-    mine = lax.dynamic_slice_in_dim(relayout, sub * BLOCK, BLOCK, axis=1)
-    own = (mine // BLOCK).reshape(1, 2 * BLOCK)
-    rt = relayout.reshape(2, SUBS, BLOCK).transpose(2, 1, 0).reshape(BLOCK, 2 * SUBS)
-    places = sub * BLOCK + jnp.arange(BLOCK, dtype=jnp.int32)
-    offsets = (neighbours - places[None, :, None]).transpose(0, 2, 1).reshape(8, BLOCK)
-    meta = jnp.concatenate([offsets, ownership, jnp.zeros((6, BLOCK), jnp.int32)], axis=0)
-    meta = jnp.pad(meta, ((0, 0), (0, 128 - BLOCK))).astype(BF16)
+    pairs = relayout.reshape(2, SUBS // 2, 2 * BLOCK).transpose(1, 0, 2)
     vmem = pl.BlockSpec(memory_space=pltpu.VMEM)
-    hbm = pl.BlockSpec(memory_space=pl.ANY)
+    hbm = pl.BlockSpec(memory_space=pltpu.HBM)
     dma = pltpu.SemaphoreType.DMA
-    return pl.pallas_call(
+    parts = pl.pallas_call(
         kernel,
         out_shape=(
-            jax.ShapeDtypeStruct((2, BLOCK, UNKNOWNS), F32),
-            jax.ShapeDtypeStruct((2, BLOCK, INTERFACE), F32),
-            jax.ShapeDtypeStruct((RES, HORIZON), F32),
+            pltpu.VMEM((2, BLOCK, UNKNOWNS), F32),
+            pltpu.VMEM((2, BLOCK, INTERFACE), F32),
+            pltpu.VMEM((RES, HORIZON), F32),
         ),
-        in_specs=[hbm, hbm, hbm, vmem, vmem, vmem, vmem],
-        out_specs=(vmem, vmem, vmem),
+        in_specs=[hbm] * 7,
+        out_specs=(vmem,) * 3,
         scratch_shapes=[
             pltpu.VMEM((2, BLOCK, UNKNOWNS), BF16),
             pltpu.VMEM((2, UNKNOWNS, UNKNOWNS), BF16),
-            pltpu.VMEM((2, UNKNOWNS, INTERFACE), BF16),
+            pltpu.VMEM((2, INTERFACE, UNKNOWNS), BF16),
             pltpu.VMEM((2 * BLOCK, UNKNOWNS), F32),
+            pltpu.VMEM((2, LANES, UNKNOWNS), BF16),
+            pltpu.VMEM((SUBS // 2, 2, 2 * BLOCK), jnp.int32),
+            pltpu.VMEM((2, 4, BLOCK), jnp.int32),
+            pltpu.VMEM((2, BLOCK), jnp.int32),
+            pltpu.VMEM((RES, HORIZON), F32),
+            pltpu.VMEM((16, 128), BF16),
             pltpu.VMEM((2, INTERFACE, UNKNOWNS), BF16),
             pltpu.VMEM((SUBS + 2 * REACH, 2, LANES), BF16),
             pltpu.VMEM((SUBS, SLAB, 2, LANES), BF16),
@@ -458,21 +493,35 @@
             pltpu.VMEM((128, 128), BF16),
             pltpu.VMEM((128, 128), BF16),
             pltpu.VMEM((2, LANES, LANES), BF16),
-            pltpu.VMEM((2, LANES, UNKNOWNS), BF16),
             pltpu.VMEM((2, ROWS, LANES), F32),
             pltpu.VMEM((2, ROWS, LANES), BF16),
             pltpu.VMEM((2, 128, LANES), F32),
             pltpu.VMEM((2, BLOCK, LANES), F32),
             pltpu.VMEM((2, 8, 8, 128), F32),
             pltpu.VMEM((2, 32, 8, 128), F32),
-            dma((6,)),
+            dma((10,)),
             dma, dma, dma, dma, dma, dma,
             dma((2,)), dma((2,)), dma((2,)), dma((2,)),
         ],
         compiler_params=pltpu.CompilerParams(
-            collective_id=0, has_side_effects=True, vmem_limit_bytes=48 * 1024 * 1024
+            collective_id=0, has_side_effects=True, vmem_limit_bytes=VMEM_LIMIT
         ),
-    )(cost_terms, coupling, solve_factor, own, rt, meta, capacity)
+    )(
+        cost_terms, coupling.transpose(0, 2, 1), solve_factor, pairs,
+        neighbours.transpose(0, 2, 1), ownership, capacity,
+    )
+    return pl.pallas_call(
+        write_out,
+        out_shape=(
+            jax.ShapeDtypeStruct((2, BLOCK, UNKNOWNS), F32),
+            jax.ShapeDtypeStruct((2, BLOCK, INTERFACE), F32),
+            jax.ShapeDtypeStruct((RES, HORIZON), F32),
+        ),
+        in_specs=[vmem] * 3,
+        out_specs=(hbm,) * 3,
+        scratch_shapes=[dma((3,))],
+        compiler_params=pltpu.CompilerParams(vmem_limit_bytes=1024 * 1024),
+    )(*parts)
 
 
 def solution(mesh):

time: 65.5 us -> 55.1 us (0.84)
  local copies, waits for them, and re-layouts: 7.79 us -> 0 us
  other arithmetic: 2.21 us -> 0 us
    unnamed x10 -> x0, local copies, waits for them, and re-layouts: 6.64 us -> none
    another operation x2 -> x0, other arithmetic: 1.38 us -> none
    reshape x4 -> x0, local copies, waits for them, and re-layouts: 1.06 us -> none  [the longest x3 0.98 us: on_device(): relayout.reshape(2, SUBS, BLOCK).transpose(2, 1, 0).reshape(BLOCK, 2 * SUBS)]
    select_n x1 -> x0, other arithmetic: 0.76 us -> none  [on_device(): own = (mine // BLOCK).reshape(1, 2 * BLOCK)]
    pallas_call x1 -> x2, Pallas kernels: 54.4 us -> 54.4 us  [the longest x1 53.6 us: on_device(): pl.pallas_call(kernel, out_shape=(pltpu.VMEM((2, BLOCK, UNKNOWNS), F32),...]
where the time goes in v1:
time: 55.1 us; the launch traced here: 55 us
  Pallas kernels  54.4 us (99%)
  between operations  0.64 us (1%)
    pallas_call x1, Pallas kernels, on_device(): pl.pallas_call(kernel, out_shape=(pltpu.VMEM((2, BLOCK, UNKNOWNS), F32),...  53.6 us

profile of v1, /device:TPU:1, one launch (start us, length us, event | category | flops | bytes accessed | tf_op | source)
XLA Modules:
  0.0 55.0 jit_solution(17377332920642660226)
XLA Ops:
  0.6 53.6 %shard_map.94 = (f32[2,64,768]{2,1,0:T(8,128)S(1)}, f32[2,64,192]{2,1,0:T(8,128)S(1)}, f32[16,48]{1,0:T(8,128)S(1)}) custom-call(bf16[2,64,768]{2,1,0:T(8,128)(2,1)} %cost.1, bf16[2,192,768]{2,1,0:T(8,128)(2,1)} %bitcast.5, bf16[2,768,768]{2,1,0:T(8,128)(2,1)} %solve.1, s32[32,2,128]{2,1,0:T(2,128)} %bitcast.6, s32[2,4,64]{2,1,0:T(4,128)} %bitcast.7, ...), custom_call_target="tpu_custom_call" | custom-call | tf_op jit(solution)/shard_map/pallas_call | solution.py:464
  54.2 0.8 %shard_map.95 = (f32[2,64,768]{2,1,0:T(8,128)}, f32[2,64,192]{2,1,0:T(8,128)}, f32[16,48]{1,0:T(8,128)}) custom-call(f32[2,64,768]{2,1,0:T(8,128)S(1)} %get-tuple-element.6.plan, f32[2,64,192]{2,1,0:T(8,128)S(1)} %get-tuple-element.7.price, f32[16,48]{1,0:T(8,128)S(1)} %get-tuple-element.8.dual), custom_call_target="tpu_custom_call" | custom-call | tf_op jit(solution)/shard_map/pallas_call | solution.py:513

commit v2 on v1

v2 whole, which is shorter than its diff:
```python
import math

import jax
import jax.numpy as jnp
from jax import lax
from jax.experimental import pallas as pl
from jax.experimental.pallas import tpu as pltpu
from jax.sharding import PartitionSpec as P

MESH = pl.DeviceIdType.MESH
F32, BF16 = jnp.float32, jnp.bfloat16
HORIZON, UNKNOWNS, INTERFACE, BLOCK = 48, 768, 192, 64
RES, SUBS, DISTS = 16, 64, 4
PAIRS = SUBS // 2
REACH = 2
SLAB = 2 * REACH + 1
PAIR = 2 * BLOCK
ROWS = SLAB * PAIR
OWN = REACH * PAIR
LANES = 256
STEP = 0.3
PEERS = SUBS - 1
OTHERS = 27
VMEM_LIMIT = 67043328 - 700 * 1024


def dot(a, b):
    return jnp.dot(a, b, preferred_element_type=F32)


def dot_ta(a, b):
    return lax.dot_general(a, b, (((0,), (0,)), ((), ())), preferred_element_type=F32)


def dot_tb(a, b):
    return lax.dot_general(a, b, (((1,), (1,)), ((), ())), preferred_element_type=F32)


def iota(shape, dim):
    return lax.broadcasted_iota(jnp.int32, shape, dim)


def folded(part):
    return jnp.concatenate([part[0:8, 0:64], part[8:16, 0:64]], axis=1)


def unfolded(part):
    return jnp.concatenate([part[:, 0:64], part[:, 64:128]], axis=0)


def kernel(
    cost, coup, solve, rel_h, near_h, owner_h, cap_h,
    plan_o, price_o, dual_o,
    X, S, C, cs, vfull, rel, near_in, owner_in, cap, meta, cts, send1, recv1, send2, recv2,
    mbuf, offs, L2, lown, p4t, p5, mp, zf, zb, sacc, usum, ara, arb, aka, akb, arc, price_s, price_r,
    load_sem, s1, r1, s2, r2, sm, rm, sp, rp, sa, ra, sb, rb, ska, rka, skb, rkb, sc, rc,
):
    sub = lax.axis_index("sub")
    dist = lax.axis_index("district")
    sxy, sz = sub // 8, lax.rem(sub, 8)
    pair, side = sub // 2, lax.rem(sub, 2)

    small = [
        pltpu.make_async_copy(src, dst, load_sem.at[6 + i])
        for i, (src, dst) in enumerate(
            ((rel_h, rel), (near_h, near_in), (owner_h, owner_in), (cap_h, cap))
        )
    ]
    loads = []
    for d in range(2):
        loads.append(pltpu.make_async_copy(cost.at[d], X.at[d], load_sem.at[3 * d]))
        loads.append(pltpu.make_async_copy(solve.at[d], S.at[d], load_sem.at[3 * d + 1]))
        loads.append(pltpu.make_async_copy(coup.at[d], C.at[d], load_sem.at[3 * d + 2]))
    for copy in small + loads:
        copy.start()

    barrier = pltpu.get_barrier_semaphore()

    def hello(k, _):
        pl.semaphore_signal(
            barrier, inc=1, device_id={"sub": lax.rem(sub + k, SUBS)}, device_id_type=MESH
        )
        return 0

    lax.fori_loop(1, SUBS, hello, 0)

    def hello_other(k, _):
        there = lax.rem(dist + 1 + k // 8, DISTS)
        pl.semaphore_signal(
            barrier,
            inc=1,
            device_id={"district": there, "sub": lax.rem(k, 8) * 8 + sz},
            device_id_type=MESH,
        )
        return 0

    lax.fori_loop(0, 24, hello_other, 0)
    for k in range(1, 4):
        pl.semaphore_signal(
            barrier,
            inc=1,
            device_id={"district": lax.rem(dist + k, DISTS), "sub": 2 * pair + 1 - side},
            device_id_type=MESH,
        )

    def whole(buf, send_sem, recv_sem):
        return pltpu.make_async_remote_copy(
            src_ref=buf,
            dst_ref=buf,
            send_sem=send_sem,
            recv_sem=recv_sem,
            device_id={"sub": sub},
            device_id_type=MESH,
        )

    for copy in small:
        copy.wait()
    place = iota((4, BLOCK), 1) + sub * BLOCK
    told = [near_in[d] - place for d in range(2)] + [owner_in[...], jnp.zeros((6, BLOCK), jnp.int32)]
    told = jnp.concatenate(told, axis=0).astype(F32)
    meta[...] = jnp.concatenate([told, jnp.zeros((16, BLOCK), F32)], axis=1).astype(BF16)
    mbuf[2 * REACH + side] = meta[...]
    here = rel[pair]
    here = jnp.where(side == 0, here[:, 0:BLOCK], here[:, BLOCK:PAIR]) // BLOCK
    own_block = jnp.concatenate([here[0:1], here[1:2]], axis=1)

    first = []
    for d in range(2):
        for copy in loads[3 * d : 3 * d + 3]:
            copy.wait()
        cs_d = dot(X[d], S[d])
        cs[d * BLOCK : (d + 1) * BLOCK] = cs_d
        first.append(dot_tb((-cs_d).astype(BF16), C[d]).astype(BF16))
    first = jnp.concatenate(first, axis=0)
    first = jnp.concatenate([first, jnp.zeros((2 * BLOCK, LANES - INTERFACE), BF16)], axis=1)
    lane = iota((2 * BLOCK, 2 * BLOCK), 1)
    row = iota((2 * BLOCK, 2 * BLOCK), 0)
    to_dest = jnp.where(own_block + BLOCK * (lane // BLOCK) == row, 1.0, 0.0).astype(BF16)
    eye = jnp.where(lane == row, 1.0, 0.0).astype(BF16)
    sorted_rows = dot(to_dest, first).astype(BF16)
    for d in range(2):
        send1[d, 0:REACH] = jnp.zeros((REACH, 2, LANES), BF16)
        send1[d, REACH + PAIRS : PAIRS + 2 * REACH] = jnp.zeros((REACH, 2, LANES), BF16)
        send1[d, REACH : REACH + PAIRS] = sorted_rows[d * BLOCK : (d + 1) * BLOCK].reshape(
            PAIRS, 2, LANES
        )

    pl.semaphore_wait(barrier, PEERS + OTHERS)

    for k in range(2 * SLAB):
        a, e = k // 2, k % 2

        def meta_copy():
            pltpu.make_async_remote_copy(
                src_ref=meta,
                dst_ref=mbuf.at[4 * REACH - 2 * a + side],
                send_sem=sm,
                recv_sem=rm,
                device_id={"sub": 2 * lax.rem(pair + a - REACH + PAIRS, PAIRS) + e},
                device_id_type=MESH,
            ).start()

        if a == REACH:
            pl.when(side != e)(meta_copy)
        else:
            meta_copy()

    def slot_of(device):
        return lax.rem(device, 2) * PAIRS + device // 2

    def send_slab(k, _):
        peer = lax.rem(sub + k, SUBS)
        pltpu.make_async_remote_copy(
            src_ref=send1.at[lax.rem(peer, 2), pl.ds(peer // 2, SLAB)],
            dst_ref=recv1.at[slot_of(sub)],
            send_sem=s1,
            recv_sem=r1,
            device_id={"sub": peer},
            device_id_type=MESH,
        ).start()
        return 0

    lax.fori_loop(1, SUBS, send_slab, 0)
    recv1[slot_of(sub)] = send1[side, pl.ds(pair, SLAB)]

    back_at = 4 * (own_block // 2) + 2 * (lane // BLOCK) + lax.rem(own_block, 2)
    p5[...] = dot_ta(jnp.where(back_at == row, 1.0, 0.0).astype(BF16), eye).astype(BF16)
    for d in range(2):
        cts_d = dot(C[d], S[d]).astype(BF16)
        cts[d] = cts_d
        m_d = dot_tb(cts_d, C[d])
        mp[d] = jnp.zeros((LANES, LANES), BF16)
        mp[d, 0:INTERFACE, 0:INTERFACE] = (-STEP * m_d).astype(BF16)
        ri = iota((LANES - INTERFACE, LANES - 128), 0)
        li = iota((LANES - INTERFACE, LANES - 128), 1)
        shift = jnp.where(li - (INTERFACE - 128) == ri + RES, 1.0, 0.0)
        mp[d, INTERFACE:LANES, 128:LANES] = shift.astype(BF16)
        vfull[d, 0:INTERFACE] = cts_d

    by_pair = rel[...].reshape(SUBS, PAIR)
    si, sj = iota((SUBS, SUBS), 0), iota((SUBS, SUBS), 1)
    pick = jnp.where((si // 2 == sj // 2) & (lax.rem(si, 2) == side), 1.0, 0.0).astype(BF16)

    def turned(values):
        flat = dot_ta(values.astype(F32).astype(BF16), pick)
        return jnp.concatenate([flat[0:BLOCK], flat[BLOCK:PAIR]], axis=1).astype(jnp.int32)

    block_of, place_in = turned(by_pair // BLOCK), turned(lax.rem(by_pair, BLOCK))
    odd = lax.rem(iota((1, PAIR), 1), 2)

    def place_map(a):
        hit = block_of == 2 * (pair + a - REACH) + odd
        at = jnp.sum(jnp.where(hit, place_in + 1, 0), axis=0, keepdims=True) - 1
        at = jnp.where(at >= 0, at + BLOCK * odd, -1)
        return jnp.where(at == row, 1.0, 0.0).astype(BF16)

    p4t[...] = dot_ta(place_map(REACH), eye).astype(BF16)

    whole(mbuf.at[pl.ds(0, 2 * SLAB - 1)], sm, rm).wait_recv()
    eye64 = jnp.where(
        iota((BLOCK, 128), 0) == iota((BLOCK, 128), 1), 1.0, 0.0
    ).astype(BF16)
    for m in range(2 * SLAB):
        cols = dot_tb(eye64, mbuf[m])
        top = m * BLOCK
        offs[top : top + BLOCK, 0:4] = jnp.where(side == 0, cols[:, 0:4], cols[:, 4:8])
        offs[top : top + BLOCK, 4:5] = jnp.where(side == 0, cols[:, 8:9], cols[:, 9:10])
    diff = (iota((LANES, LANES), 1) - iota((LANES, LANES), 0)).astype(F32)
    for i in range(3):
        cols = offs[192 * i : 192 * i + 256]
        near = jnp.where(diff == 0.0, 1.0, 0.0)
        for k in range(4):
            near = near - jnp.where(diff == cols[:, k : k + 1], 0.25, 0.0)
        near = near.astype(BF16)
        L2[i] = dot(near, near)[32:224].astype(BF16)
        if i == 1:
            lown[...] = near[64:192]

    sacc[...] = jnp.zeros((256, LANES), F32)
    whole(recv1.at[pl.ds(0, PEERS)], s1, r1).wait_recv()
    lane_e = iota((PAIR, 128), 1) - (INTERFACE - 128)
    for a in range(SLAB):
        arrived = recv1[:, a].reshape(2 * SUBS, LANES)
        part = dot(place_map(a), arrived)
        top = a * PAIR
        owner = offs[top : top + PAIR, 4:5].astype(jnp.int32)
        mark = jnp.where((lane_e == owner) & (lane_e >= 0) & (lane_e < RES), 1.0, 0.0)
        low, high = part[:, 0:128], part[:, 128:LANES] + mark
        zf[top : top + PAIR, 0:128] = low
        zf[top : top + PAIR, 128:LANES] = high
        zb[top : top + PAIR, 0:128] = low.astype(BF16)
        zb[top : top + PAIR, 128:LANES] = high.astype(BF16)
    sacc[32:224] = zf[224:416]
    usum[...] = jnp.zeros((PAIR, LANES), F32)
    flow_map = mp.at[side]

    def half(i):
        u = dot(L2[i], zb[192 * i : 192 * i + 256])
        if i == 1:
            usum[...] += u[32:160]
        return u.astype(BF16)

    def advance(i, u):
        at = 32 + 192 * i
        z = zf[at : at + 192] + dot(u, flow_map[...])
        zf[at : at + 192] = z
        zb[at : at + 192] = z.astype(BF16)
        if i == 1:
            sacc[32:224] += z

    def step():
        us = [half(i) for i in range(3)]
        for i, u in enumerate(us):
            advance(i, u)

    def full_step(_, carry):
        step()
        return carry

    def own_part(with_lanes):
        marked = zb[OWN : OWN + PAIR, INTERFACE : INTERFACE + RES]
        return dot_ta(marked, with_lanes)

    def to_z(buf, t, send_sem, recv_sem, first_k, stride):
        def go(k, _):
            z = lax.rem(sz + first_k + stride * k, 8)
            pltpu.make_async_remote_copy(
                src_ref=buf.at[t, sz],
                dst_ref=buf.at[t, sz],
                send_sem=send_sem.at[t],
                recv_sem=recv_sem.at[t],
                device_id={"sub": sxy * 8 + z},
                device_id_type=MESH,
            ).start()
            return 0

        lax.fori_loop(0, 8 // stride - 1, go, 0)

    def start_b(t):
        here_b = dist * 8 + sxy

        def go(k, _):
            there = lax.rem(here_b + k, 32)
            pltpu.make_async_remote_copy(
                src_ref=arb.at[t, here_b],
                dst_ref=arb.at[t, here_b],
                send_sem=sb.at[t],
                recv_sem=rb.at[t],
                device_id={"district": there // 8, "sub": lax.rem(there, 8) * 8 + sz},
                device_id_type=MESH,
            ).start()
            return 0

        lax.fori_loop(1, 32, go, 0)

    def all_of(buf, t, count, send_sem, recv_sem):
        return whole(buf.at[t, pl.ds(0, count)], send_sem.at[t], recv_sem.at[t])

    def reduce_a(t, part):
        ara[t, sz] = folded(part)
        to_z(ara, t, sa, ra, 1, 1)

    def reduce_b(t):
        all_of(ara, t, 7, sa, ra).wait_recv()
        arb[t, dist * 8 + sxy] = jnp.sum(ara[t], axis=0)
        start_b(t)

    def reduce_end(t):
        all_of(arb, t, 31, sb, rb).wait_recv()
        return unfolded(jnp.sum(arb[t], axis=0))

    lax.fori_loop(0, 3, full_step, 0)
    reduce_a(0, own_part(zb[OWN : OWN + PAIR, 0:128]))
    marks = zb[OWN : OWN + PAIR, INTERFACE:LANES]
    aka[0, sz // 2] = folded(own_part(marks))

    def go_k(k, _):
        z = lax.rem(sz + 2 + 2 * k, 8)
        pltpu.make_async_remote_copy(
            src_ref=aka.at[0, sz // 2],
            dst_ref=aka.at[0, sz // 2],
            send_sem=ska,
            recv_sem=rka,
            device_id={"sub": sxy * 8 + z},
            device_id_type=MESH,
        ).start()
        return 0

    lax.fori_loop(0, 3, go_k, 0)
    near_marks = dot(lown[...], zb[192:448])[:, INTERFACE:LANES].astype(BF16)
    step()
    step()
    step()

    u = half(1)
    prices = (STEP * usum[...]).astype(BF16)
    back = jnp.concatenate([prices[:, 0:INTERFACE], marks], axis=1)
    send2[...] = dot(p4t[...], back).astype(BF16).reshape(SUBS, 2, LANES)

    def send_row(k, _):
        peer = lax.rem(sub + k, SUBS)
        pltpu.make_async_remote_copy(
            src_ref=send2.at[slot_of(peer)],
            dst_ref=recv2.at[sub],
            send_sem=s2,
            recv_sem=r2,
            device_id={"sub": peer},
            device_id_type=MESH,
        ).start()
        return 0

    lax.fori_loop(1, SUBS, send_row, 0)
    recv2[sub] = send2[slot_of(sub)]

    advance(1, u)
    reduce_a(1, own_part(zb[OWN : OWN + PAIR, 0:128]))
    price0 = dot(lown[...], sacc[...].astype(BF16))[:, 0:INTERFACE]

    reduce_b(0)
    whole(aka.at[0, pl.ds(0, 3)], ska, rka).wait_recv()
    akb[0, sxy] = jnp.sum(aka[0], axis=0)

    def go_kb(k, _):
        xy = lax.rem(sxy + k, 8)
        pltpu.make_async_remote_copy(
            src_ref=akb.at[0, sxy],
            dst_ref=akb.at[0, sxy],
            send_sem=skb,
            recv_sem=rkb,
            device_id={"sub": xy * 8 + sz},
            device_id_type=MESH,
        ).start()
        return 0

    lax.fori_loop(1, 8, go_kb, 0)
    reduce_b(1)
    capacity = cap[...]
    scale = 1.0 / math.sqrt(DISTS * 2 * SUBS * BLOCK / (2 * RES))
    duals = (reduce_end(0)[:, 0:HORIZON] - capacity) * scale
    wide = jnp.concatenate([duals, jnp.zeros((RES, INTERFACE - HORIZON), F32)], axis=1)

    binom = (1.0, 3.0, 3.0, 1.0)
    in_price = (1.0, -0.9, 0.27, -0.027)
    in_flow = (-1.0, 0.9, -0.27, 0.027)
    in_sum = (-4.0, 1.8, -0.36, 0.027)

    def powers_of(m_ref, count):
        powers = [wide]
        for _ in range(count):
            powers.append(
                dot(powers[-1].astype(BF16), m_ref[0:INTERFACE, 0:INTERFACE]) * (-1.0 / STEP)
            )
        return powers

    def stack(powers, weights):
        return jnp.concatenate(
            [p * (w / b) for p, w, b in zip(powers, weights, binom)], axis=0
        ).astype(BF16)

    powers = powers_of(flow_map, 4)
    whole(akb.at[0, pl.ds(0, 7)], skb, rkb).wait_recv()
    unit = unfolded(jnp.sum(akb[0], axis=0)).astype(BF16)
    here_c = dist * 2 + side
    arc[here_c] = folded(dot(unit, stack(powers[1:], in_flow))[:, 0:128])

    def go_c(k, _):
        there = lax.rem(here_c + k, 8)
        pltpu.make_async_remote_copy(
            src_ref=arc.at[here_c],
            dst_ref=arc.at[here_c],
            send_sem=sc,
            recv_sem=rc,
            device_id={"district": there // 2, "sub": 2 * pair + lax.rem(there, 2)},
            device_id_type=MESH,
        ).start()
        return 0

    lax.fori_loop(1, 8, go_c, 0)
    final_price = STEP * (price0 + dot(near_marks, stack(powers[1:], in_sum)))
    halves = [final_price[0:BLOCK], final_price[BLOCK:PAIR]]
    price_s[...] = jnp.where(side == 0, halves[1], halves[0])
    price_copy = pltpu.make_async_remote_copy(
        src_ref=price_s,
        dst_ref=price_r,
        send_sem=sp,
        recv_sem=rp,
        device_id={"sub": 2 * pair + 1 - side},
        device_id_type=MESH,
    )
    price_copy.start()
    price_o[side] = jnp.where(side == 0, halves[0], halves[1])
    for d in range(2):
        powers_d = powers_of(mp.at[d], 3)
        vfull[d, INTERFACE:LANES] = dot(stack(powers_d, in_price), cts[d]).astype(BF16)

    whole(recv2.at[pl.ds(0, PEERS)], s2, r2).wait_recv()
    mine = dot(p5[...], recv2[...].reshape(2 * SUBS, LANES)).astype(BF16)
    for d in range(2):
        at = d * BLOCK
        plan_o[d] = -(cs[at : at + BLOCK] + dot(mine[at : at + BLOCK], vfull[d]))

    price_copy.wait_recv()
    price_o[1 - side] = price_r[...]
    draws0 = reduce_end(1)[:, 0:HORIZON]
    whole(arc.at[pl.ds(0, 7)], sc, rc).wait_recv()
    draws1 = unfolded(jnp.sum(arc[...], axis=0))[:, 0:HORIZON]
    dual_o[...] = duals + (draws0 + draws1 - capacity) * scale

    whole(mbuf.at[pl.ds(0, 2 * SLAB - 1)], sm, rm).wait_send()
    whole(recv1.at[pl.ds(0, PEERS)], s1, r1).wait_send()
    whole(recv2.at[pl.ds(0, PEERS)], s2, r2).wait_send()
    for t in range(2):
        all_of(ara, t, 7, sa, ra).wait_send()
        all_of(arb, t, 31, sb, rb).wait_send()
    whole(aka.at[0, pl.ds(0, 3)], ska, rka).wait_send()
    whole(akb.at[0, pl.ds(0, 7)], skb, rkb).wait_send()
    whole(arc.at[pl.ds(0, 7)], sc, rc).wait_send()
    price_copy.wait_send()


def write_out(plan, price, dual, plan_o, price_o, dual_o, sems):
    copies = [
        pltpu.make_async_copy(src, dst, sems.at[i])
        for i, (src, dst) in enumerate(((plan, plan_o), (price, price_o), (dual, dual_o)))
    ]
    for copy in copies:
        copy.start()
    for copy in copies:
        copy.wait()


def on_device(cost_terms, neighbours, relayout, ownership, capacity, coupling, solve_factor):
    pairs = relayout.reshape(2, SUBS // 2, 2 * BLOCK).transpose(1, 0, 2)
    vmem = pl.BlockSpec(memory_space=pltpu.VMEM)
    hbm = pl.BlockSpec(memory_space=pltpu.HBM)
    dma = pltpu.SemaphoreType.DMA
    parts = pl.pallas_call(
        kernel,
        out_shape=(
            pltpu.VMEM((2, BLOCK, UNKNOWNS), F32),
            pltpu.VMEM((2, BLOCK, INTERFACE), F32),
            pltpu.VMEM((RES, HORIZON), F32),
        ),
        in_specs=[hbm] * 7,
        out_specs=(vmem,) * 3,
        scratch_shapes=[
            pltpu.VMEM((2, BLOCK, UNKNOWNS), BF16),
            pltpu.VMEM((2, UNKNOWNS, UNKNOWNS), BF16),
            pltpu.VMEM((2, INTERFACE, UNKNOWNS), BF16),
            pltpu.VMEM((2 * BLOCK, UNKNOWNS), F32),
            pltpu.VMEM((2, LANES, UNKNOWNS), BF16),
            pltpu.VMEM((SUBS // 2, 2, 2 * BLOCK), jnp.int32),
            pltpu.VMEM((2, 4, BLOCK), jnp.int32),
            pltpu.VMEM((2, BLOCK), jnp.int32),
            pltpu.VMEM((RES, HORIZON), F32),
            pltpu.VMEM((16, 128), BF16),
            pltpu.VMEM((2, INTERFACE, UNKNOWNS), BF16),
            pltpu.VMEM((2, PAIRS + 2 * REACH, 2, LANES), BF16),
            pltpu.VMEM((SUBS, SLAB, 2, LANES), BF16),
            pltpu.VMEM((SUBS, 2, LANES), BF16),
            pltpu.VMEM((SUBS, 2, LANES), BF16),
            pltpu.VMEM((2 * SLAB, 16, 128), BF16),
            pltpu.VMEM((ROWS, 8), F32),
            pltpu.VMEM((3, 192, 256), BF16),
            pltpu.VMEM((PAIR, 256), BF16),
            pltpu.VMEM((128, 128), BF16),
            pltpu.VMEM((128, 128), BF16),
            pltpu.VMEM((2, LANES, LANES), BF16),
            pltpu.VMEM((ROWS, LANES), F32),
            pltpu.VMEM((ROWS, LANES), BF16),
            pltpu.VMEM((256, LANES), F32),
            pltpu.VMEM((PAIR, LANES), F32),
            pltpu.VMEM((2, 8, 8, 128), F32),
            pltpu.VMEM((2, 32, 8, 128), F32),
            pltpu.VMEM((1, 4, 8, 128), F32),
            pltpu.VMEM((1, 8, 8, 128), F32),
            pltpu.VMEM((8, 8, 128), F32),
            pltpu.VMEM((BLOCK, INTERFACE), F32),
            pltpu.VMEM((BLOCK, INTERFACE), F32),
            dma((10,)),
            dma, dma, dma, dma, dma, dma, dma, dma,
            dma((2,)), dma((2,)), dma((2,)), dma((2,)),
            dma, dma, dma, dma, dma, dma,
        ],
        compiler_params=pltpu.CompilerParams(
            collective_id=0, has_side_effects=True, vmem_limit_bytes=VMEM_LIMIT
        ),
    )(
        cost_terms, coupling.transpose(0, 2, 1), solve_factor, pairs,
        neighbours.transpose(0, 2, 1), ownership, capacity,
    )
    return pl.pallas_call(
        write_out,
        out_shape=(
            jax.ShapeDtypeStruct((2, BLOCK, UNKNOWNS), F32),
            jax.ShapeDtypeStruct((2, BLOCK, INTERFACE), F32),
            jax.ShapeDtypeStruct((RES, HORIZON), F32),
        ),
        in_specs=[vmem] * 3,
        out_specs=(hbm,) * 3,
        scratch_shapes=[dma((3,))],
        compiler_params=pltpu.CompilerParams(vmem_limit_bytes=1024 * 1024),
    )(*parts)


def solution(mesh):
    placed = (
        P("district", "sub", None),
        P("district", "sub", None),
        P("district", None),
        P("district", "sub"),
        P(),
        P("district", None, None),
        P("district", None, None),
    )
    return jax.shard_map(
        on_device,
        mesh=mesh,
        in_specs=placed,
        out_specs=(P("district", "sub", None), P("district", "sub", None), P()),
        check_vma=False,
    )
```

time: 55.1 us -> 44.2 us (0.80)
  Pallas kernels: 54.4 us -> 43.4 us
    pallas_call x1, Pallas kernels: 53.6 us -> 42.6 us  [on_device(): pl.pallas_call(kernel, out_shape=(pltpu.VMEM((2, BLOCK, UNKNOWNS), F32),...]
where the time goes in v2:
time: 44.2 us; the launch traced here: 44.1 us
  Pallas kernels  43.4 us (98%)
  between operations  0.64 us (1%)
    pallas_call x1, Pallas kernels, on_device(): pl.pallas_call(kernel, out_shape=(pltpu.VMEM((2, BLOCK, UNKNOWNS), F32),...  42.6 us

profile of v2, /device:TPU:1, one launch (start us, length us, event | category | flops | bytes accessed | tf_op | source)
XLA Modules:
  0.0 44.1 jit_solution(2656248043881005646)
XLA Ops:
  0.6 42.6 %shard_map.94 = (f32[2,64,768]{2,1,0:T(8,128)S(1)}, f32[2,64,192]{2,1,0:T(8,128)S(1)}, f32[16,48]{1,0:T(8,128)S(1)}) custom-call(bf16[2,64,768]{2,1,0:T(8,128)(2,1)} %cost.1, bf16[2,192,768]{2,1,0:T(8,128)(2,1)} %bitcast.5, bf16[2,768,768]{2,1,0:T(8,128)(2,1)} %solve.1, s32[32,2,128]{2,1,0:T(2,128)} %bitcast.6, s32[2,4,64]{2,1,0:T(4,128)} %bitcast.7, ...), custom_call_target="tpu_custom_call" | custom-call | tf_op jit(solution)/shard_map/pallas_call | solution.py:497
  43.3 0.8 %shard_map.95 = (f32[2,64,768]{2,1,0:T(8,128)}, f32[2,64,192]{2,1,0:T(8,128)}, f32[16,48]{1,0:T(8,128)}) custom-call(f32[2,64,768]{2,1,0:T(8,128)S(1)} %get-tuple-element.6.plan, f32[2,64,192]{2,1,0:T(8,128)S(1)} %get-tuple-element.7.price, f32[16,48]{1,0:T(8,128)S(1)} %get-tuple-element.8.dual), custom_call_target="tpu_custom_call" | custom-call | tf_op jit(solution)/shard_map/pallas_call | solution.py:552

commit v3 on v2

--- a/solution.py
+++ b/solution.py
@@ -40,6 +40,15 @@
     return lax.broadcasted_iota(jnp.int32, shape, dim)
 
 
+def offsets_by_hops():
+    def hops(at):
+        x, y, z = at
+        return min(x, 4 - x) + 2 * y + min(z, 8 - z)
+
+    every = [(x, y, z) for z in range(8) for x in range(4) for y in range(2)]
+    return sorted(every, key=lambda at: (-hops(at), at))
+
+
 def folded(part):
     return jnp.concatenate([part[0:8, 0:64], part[8:16, 0:64]], axis=1)
 
@@ -75,33 +84,27 @@
         copy.start()
 
     barrier = pltpu.get_barrier_semaphore()
-
-    def hello(k, _):
-        pl.semaphore_signal(
-            barrier, inc=1, device_id={"sub": lax.rem(sub + k, SUBS)}, device_id_type=MESH
-        )
-        return 0
-
-    lax.fori_loop(1, SUBS, hello, 0)
-
-    def hello_other(k, _):
-        there = lax.rem(dist + 1 + k // 8, DISTS)
-        pl.semaphore_signal(
-            barrier,
-            inc=1,
-            device_id={"district": there, "sub": lax.rem(k, 8) * 8 + sz},
-            device_id_type=MESH,
-        )
-        return 0
-
-    lax.fori_loop(0, 24, hello_other, 0)
-    for k in range(1, 4):
-        pl.semaphore_signal(
-            barrier,
-            inc=1,
-            device_id={"district": lax.rem(dist + k, DISTS), "sub": 2 * pair + 1 - side},
-            device_id_type=MESH,
-        )
+    sx, sy = sub // 16, lax.rem(sxy, 2)
+    x_at = [16 * lax.rem(sx + k, 4) for k in range(4)]
+    y_at = [8 * lax.rem(sy + k, 2) for k in range(2)]
+    z_at = [lax.rem(sz + k, 8) for k in range(8)]
+    xy_at = {(x, y): x_at[x] + y_at[y] for x in range(4) for y in range(2)}
+    dist_at = [lax.rem(dist + k, DISTS) for k in range(DISTS)]
+    order = offsets_by_hops()
+    peers = [xy_at[x, y] + z_at[z] for x, y, z in order[:-1]]
+    level = [xy_at[x, y] for x, y, z in order if z == 0]
+    ring = [z_at[k] for k in (4, 3, 5, 2, 6, 1, 7)]
+
+    def hello(device):
+        pl.semaphore_signal(barrier, inc=1, device_id=device, device_id_type=MESH)
+
+    for peer in peers:
+        hello({"sub": peer})
+    for at in level:
+        for k in range(1, DISTS):
+            hello({"district": dist_at[k], "sub": at + sz})
+    for k in range(1, DISTS):
+        hello({"district": dist_at[k], "sub": 2 * pair + 1 - side})
 
     def whole(buf, send_sem, recv_sem):
         return pltpu.make_async_remote_copy(
@@ -168,19 +171,16 @@
     def slot_of(device):
         return lax.rem(device, 2) * PAIRS + device // 2
 
-    def send_slab(k, _):
-        peer = lax.rem(sub + k, SUBS)
+    slot = slot_of(sub)
+    for peer in peers:
         pltpu.make_async_remote_copy(
             src_ref=send1.at[lax.rem(peer, 2), pl.ds(peer // 2, SLAB)],
-            dst_ref=recv1.at[slot_of(sub)],
+            dst_ref=recv1.at[slot],
             send_sem=s1,
             recv_sem=r1,
             device_id={"sub": peer},
             device_id_type=MESH,
         ).start()
-        return 0
-
-    lax.fori_loop(1, SUBS, send_slab, 0)
     recv1[slot_of(sub)] = send1[side, pl.ds(pair, SLAB)]
 
     back_at = 4 * (own_block // 2) + 2 * (lane // BLOCK) + lax.rem(own_block, 2)
@@ -281,9 +281,8 @@
         marked = zb[OWN : OWN + PAIR, INTERFACE : INTERFACE + RES]
         return dot_ta(marked, with_lanes)
 
-    def to_z(buf, t, send_sem, recv_sem, first_k, stride):
-        def go(k, _):
-            z = lax.rem(sz + first_k + stride * k, 8)
+    def to_z(buf, t, send_sem, recv_sem):
+        for z in ring:
             pltpu.make_async_remote_copy(
                 src_ref=buf.at[t, sz],
                 dst_ref=buf.at[t, sz],
@@ -292,33 +291,28 @@
                 device_id={"sub": sxy * 8 + z},
                 device_id_type=MESH,
             ).start()
-            return 0
-
-        lax.fori_loop(0, 8 // stride - 1, go, 0)
 
     def start_b(t):
         here_b = dist * 8 + sxy
-
-        def go(k, _):
-            there = lax.rem(here_b + k, 32)
-            pltpu.make_async_remote_copy(
-                src_ref=arb.at[t, here_b],
-                dst_ref=arb.at[t, here_b],
-                send_sem=sb.at[t],
-                recv_sem=rb.at[t],
-                device_id={"district": there // 8, "sub": lax.rem(there, 8) * 8 + sz},
-                device_id_type=MESH,
-            ).start()
-            return 0
-
-        lax.fori_loop(1, 32, go, 0)
+        for at in level:
+            for k in (2, 1, 3, 0):
+                if k == 0 and at is level[-1]:
+                    continue
+                pltpu.make_async_remote_copy(
+                    src_ref=arb.at[t, here_b],
+                    dst_ref=arb.at[t, here_b],
+                    send_sem=sb.at[t],
+                    recv_sem=rb.at[t],
+                    device_id={"district": dist_at[k], "sub": at + sz},
+                    device_id_type=MESH,
+                ).start()
 
     def all_of(buf, t, count, send_sem, recv_sem):
         return whole(buf.at[t, pl.ds(0, count)], send_sem.at[t], recv_sem.at[t])
 
     def reduce_a(t, part):
         ara[t, sz] = folded(part)
-        to_z(ara, t, sa, ra, 1, 1)
+        to_z(ara, t, sa, ra)
 
     def reduce_b(t):
         all_of(ara, t, 7, sa, ra).wait_recv()
@@ -357,8 +351,7 @@
     back = jnp.concatenate([prices[:, 0:INTERFACE], marks], axis=1)
     send2[...] = dot(p4t[...], back).astype(BF16).reshape(SUBS, 2, LANES)
 
-    def send_row(k, _):
-        peer = lax.rem(sub + k, SUBS)
+    for peer in peers:
         pltpu.make_async_remote_copy(
             src_ref=send2.at[slot_of(peer)],
             dst_ref=recv2.at[sub],
@@ -367,9 +360,6 @@
             device_id={"sub": peer},
             device_id_type=MESH,
         ).start()
-        return 0
-
-    lax.fori_loop(1, SUBS, send_row, 0)
     recv2[sub] = send2[slot_of(sub)]
 
     advance(1, u)

time: 44.2 us -> 41.6 us (0.941)
  Pallas kernels: 43.4 us -> 40.8 us
    pallas_call x1, Pallas kernels: 42.6 us -> 40 us  [on_device(): pl.pallas_call(kernel, out_shape=(pltpu.VMEM((2, BLOCK, UNKNOWNS), F32),...]
where the time goes in v3:
time: 41.6 us; the launch traced here: 41.5 us
  Pallas kernels  40.8 us (98%)
  between operations  0.64 us (2%)
    pallas_call x1, Pallas kernels, on_device(): pl.pallas_call(kernel, out_shape=(pltpu.VMEM((2, BLOCK, UNKNOWNS), F32),...  40 us

profile of v3, /device:TPU:1, one launch (start us, length us, event | category | flops | bytes accessed | tf_op | source)
XLA Modules:
  0.0 41.5 jit_solution(5244912130691380664)
XLA Ops:
  0.6 40.0 %shard_map.94 = (f32[2,64,768]{2,1,0:T(8,128)S(1)}, f32[2,64,192]{2,1,0:T(8,128)S(1)}, f32[16,48]{1,0:T(8,128)S(1)}) custom-call(bf16[2,64,768]{2,1,0:T(8,128)(2,1)} %cost.1, bf16[2,192,768]{2,1,0:T(8,128)(2,1)} %bitcast.5, bf16[2,768,768]{2,1,0:T(8,128)(2,1)} %solve.1, s32[32,2,128]{2,1,0:T(2,128)} %bitcast.6, s32[2,4,64]{2,1,0:T(4,128)} %bitcast.7, ...), custom_call_target="tpu_custom_call" | custom-call | tf_op jit(solution)/shard_map/pallas_call | solution.py:487
  40.6 0.8 %shard_map.95 = (f32[2,64,768]{2,1,0:T(8,128)}, f32[2,64,192]{2,1,0:T(8,128)}, f32[16,48]{1,0:T(8,128)}) custom-call(f32[2,64,768]{2,1,0:T(8,128)S(1)} %get-tuple-element.6.plan, f32[2,64,192]{2,1,0:T(8,128)S(1)} %get-tuple-element.7.price, f32[16,48]{1,0:T(8,128)S(1)} %get-tuple-element.8.dual), custom_call_target="tpu_custom_call" | custom-call | tf_op jit(solution)/shard_map/pallas_call | solution.py:542

commit v4 on v3

--- a/solution.py
+++ b/solution.py
@@ -36,6 +36,16 @@
     return lax.dot_general(a, b, (((1,), (1,)), ((), ())), preferred_element_type=F32)
 
 
+def two_parts(x):
+    high = x.astype(BF16)
+    return jnp.concatenate([high, (x - high.astype(F32)).astype(BF16)], axis=0)
+
+
+def dot2(x, b):
+    out = dot(two_parts(x), b)
+    return out[: x.shape[0]] + out[x.shape[0] :]
+
+
 def iota(shape, dim):
     return lax.broadcasted_iota(jnp.int32, shape, dim)
 
@@ -62,7 +72,8 @@
     plan_o, price_o, dual_o,
     X, S, C, cs, vfull, rel, near_in, owner_in, cap, meta, cts, send1, recv1, send2, recv2,
     mbuf, offs, L2, lown, p4t, p5, mp, zf, zb, sacc, usum, ara, arb, aka, akb, arc, price_s, price_r,
-    load_sem, s1, r1, s2, r2, sm, rm, sp, rp, sa, ra, sb, rb, ska, rka, skb, rkb, sc, rc,
+
+    load_sem, s1, r1, s2, r2, sm, rm, sp, rp, sa, ra, sb, rb, ska, rka, skb, rkb, sc, rc, se, re,
 ):
     sub = lax.axis_index("sub")
     dist = lax.axis_index("district")
@@ -119,10 +130,11 @@
     for copy in small:
         copy.wait()
     place = iota((4, BLOCK), 1) + sub * BLOCK
-    told = [near_in[d] - place for d in range(2)] + [owner_in[...], jnp.zeros((6, BLOCK), jnp.int32)]
-    told = jnp.concatenate(told, axis=0).astype(F32)
-    meta[...] = jnp.concatenate([told, jnp.zeros((16, BLOCK), F32)], axis=1).astype(BF16)
-    mbuf[2 * REACH + side] = meta[...]
+    for d in range(2):
+        told = [near_in[d] - place, owner_in[d : d + 1], jnp.zeros((11, BLOCK), jnp.int32)]
+        told = jnp.concatenate(told, axis=0).astype(F32)
+        meta[d] = jnp.concatenate([told, jnp.zeros((16, BLOCK), F32)], axis=1).astype(BF16)
+    mbuf[2 * REACH + side] = meta[side]
     here = rel[pair]
     here = jnp.where(side == 0, here[:, 0:BLOCK], here[:, BLOCK:PAIR]) // BLOCK
     own_block = jnp.concatenate([here[0:1], here[1:2]], axis=1)
@@ -155,7 +167,7 @@
 
         def meta_copy():
             pltpu.make_async_remote_copy(
-                src_ref=meta,
+                src_ref=meta.at[e],
                 dst_ref=mbuf.at[4 * REACH - 2 * a + side],
                 send_sem=sm,
                 recv_sem=rm,
@@ -174,14 +186,24 @@
     slot = slot_of(sub)
     for peer in peers:
         pltpu.make_async_remote_copy(
-            src_ref=send1.at[lax.rem(peer, 2), pl.ds(peer // 2, SLAB)],
-            dst_ref=recv1.at[slot],
-            send_sem=s1,
-            recv_sem=r1,
+            src_ref=send1.at[lax.rem(peer, 2), REACH + peer // 2],
+            dst_ref=recv1.at[slot, REACH],
+            send_sem=se,
+            recv_sem=re,
             device_id={"sub": peer},
             device_id_type=MESH,
         ).start()
-    recv1[slot_of(sub)] = send1[side, pl.ds(pair, SLAB)]
+    for peer in peers:
+        for first in (0, REACH + 1):
+            pltpu.make_async_remote_copy(
+                src_ref=send1.at[lax.rem(peer, 2), pl.ds(peer // 2 + first, REACH)],
+                dst_ref=recv1.at[slot, pl.ds(first, REACH)],
+                send_sem=s1,
+                recv_sem=r1,
+                device_id={"sub": peer},
+                device_id_type=MESH,
+            ).start()
+    recv1[slot] = send1[side, pl.ds(pair, SLAB)]
 
     back_at = 4 * (own_block // 2) + 2 * (lane // BLOCK) + lax.rem(own_block, 2)
     p5[...] = dot_ta(jnp.where(back_at == row, 1.0, 0.0).astype(BF16), eye).astype(BF16)
@@ -214,17 +236,15 @@
         at = jnp.where(at >= 0, at + BLOCK * odd, -1)
         return jnp.where(at == row, 1.0, 0.0).astype(BF16)
 
-    p4t[...] = dot_ta(place_map(REACH), eye).astype(BF16)
+    own_map = place_map(REACH)
+    p4t[...] = dot_ta(own_map, eye).astype(BF16)
 
     whole(mbuf.at[pl.ds(0, 2 * SLAB - 1)], sm, rm).wait_recv()
     eye64 = jnp.where(
         iota((BLOCK, 128), 0) == iota((BLOCK, 128), 1), 1.0, 0.0
     ).astype(BF16)
     for m in range(2 * SLAB):
-        cols = dot_tb(eye64, mbuf[m])
-        top = m * BLOCK
-        offs[top : top + BLOCK, 0:4] = jnp.where(side == 0, cols[:, 0:4], cols[:, 4:8])
-        offs[top : top + BLOCK, 4:5] = jnp.where(side == 0, cols[:, 8:9], cols[:, 9:10])
+        offs[m * BLOCK : (m + 1) * BLOCK] = dot_tb(eye64, mbuf[m])
     diff = (iota((LANES, LANES), 1) - iota((LANES, LANES), 0)).astype(F32)
     for i in range(3):
         cols = offs[192 * i : 192 * i + 256]
@@ -232,12 +252,127 @@
         for k in range(4):
             near = near - jnp.where(diff == cols[:, k : k + 1], 0.25, 0.0)
         near = near.astype(BF16)
-        L2[i] = dot(near, near)[32:224].astype(BF16)
+        L2[i, 32:224] = dot(near, near)[32:224].astype(BF16)
+        L2[i, 0:32] = jnp.zeros((32, 256), BF16)
+        L2[i, 224:256] = jnp.zeros((32, 256), BF16)
         if i == 1:
             lown[...] = near[64:192]
 
+    def to_z(buf, t, send_sem, recv_sem):
+        for z in ring:
+            pltpu.make_async_remote_copy(
+                src_ref=buf.at[t, sz],
+                dst_ref=buf.at[t, sz],
+                send_sem=send_sem.at[t],
+                recv_sem=recv_sem.at[t],
+                device_id={"sub": sxy * 8 + z},
+                device_id_type=MESH,
+            ).start()
+
+    def start_b(t):
+        here_b = dist * 8 + sxy
+        for at in level:
+            for k in (2, 1, 3, 0):
+                if k == 0 and at is level[-1]:
+                    continue
+                pltpu.make_async_remote_copy(
+                    src_ref=arb.at[t, here_b],
+                    dst_ref=arb.at[t, here_b],
+                    send_sem=sb.at[t],
+                    recv_sem=rb.at[t],
+                    device_id={"district": dist_at[k], "sub": at + sz},
+                    device_id_type=MESH,
+                ).start()
+
+    def all_of(buf, t, count, send_sem, recv_sem):
+        return whole(buf.at[t, pl.ds(0, count)], send_sem.at[t], recv_sem.at[t])
+
+    def reduce_a(t, part):
+        ara[t, sz] = folded(part)
+        to_z(ara, t, sa, ra)
+
+    def reduce_b(t):
+        all_of(ara, t, 7, sa, ra).wait_recv()
+        arb[t, dist * 8 + sxy] = jnp.sum(ara[t], axis=0)
+        start_b(t)
+
+    def reduce_end(t):
+        all_of(arb, t, 31, sb, rb).wait_recv()
+        return unfolded(jnp.sum(arb[t], axis=0))
+
+    flow_map = mp.at[side]
+    owners = []
+    for a in range(SLAB):
+        owner = [mbuf[2 * a + e][4:5, 0:BLOCK].astype(F32) for e in range(2)]
+        owner = jnp.concatenate(owner, axis=1)
+        owners.append(jnp.where(iota((RES, PAIR), 0).astype(F32) == owner, 1.0, 0.0))
+    own_owners = owners[REACH]
+    half_tile = jnp.zeros((2 * RES, BLOCK), F32)
+
+    def back_step(tiles):
+        rows2 = jnp.concatenate([two_parts(t) for t in tiles], axis=1)
+        out0 = dot(rows2[:, 0:256], L2[0])
+        out1 = dot(rows2[:, 192:448], L2[1])
+        out2 = dot(rows2[:, 384:640], L2[2])
+        out1 = jnp.concatenate([half_tile, out1, half_tile], axis=1)
+        sums = [
+            out0[:, 0:128],
+            out0[:, 128:256] + out1[:, 0:128],
+            out1[:, 128:256],
+            out1[:, 256:384] + out2[:, 0:128],
+            out2[:, 128:256],
+        ]
+        return [t[0:RES] + t[RES : 2 * RES] for t in sums]
+
+    def seen_flows(weights):
+        turned_weights = dot(two_parts(weights), own_map).astype(BF16)
+        sums = dot(turned_weights, recv1[:, REACH].reshape(2 * SUBS, LANES))[:, 0:INTERFACE]
+        sums = sums[0:BLOCK] + sums[BLOCK : 2 * BLOCK]
+        return [sums[RES * j : RES * (j + 1)] for j in range(4)]
+
+    def draws_of(seen, count):
+        total = seen[count]
+        for j in reversed(range(count)):
+            total = dot2(total, flow_map[0:INTERFACE, 0:INTERFACE])
+            total = total + seen[j] * float(math.comb(count, j))
+        return total[:, 0:128]
+
+    weights, tiles = [own_owners], owners
+    for _ in range(3):
+        tiles = back_step(tiles)
+        weights.append(tiles[REACH])
+    weights = jnp.concatenate(weights, axis=0)
+    unit = dot_tb(two_parts(weights), own_owners.astype(BF16))
+    unit = unit[0:BLOCK] + unit[BLOCK : 2 * BLOCK]
+    unit = [unit[RES * j : RES * (j + 1), 0:RES] for j in range(4)]
+    aka[0, sz // 2] = folded(jnp.concatenate(unit, axis=1))
+    whole(recv1.at[pl.ds(0, PEERS), REACH], se, re).wait_recv()
+    seen = seen_flows(weights)
+    reduce_a(0, draws_of(seen, 3))
+
+    def go_k(k, _):
+        z = lax.rem(sz + 2 + 2 * k, 8)
+        pltpu.make_async_remote_copy(
+            src_ref=aka.at[0, sz // 2],
+            dst_ref=aka.at[0, sz // 2],
+            send_sem=ska,
+            recv_sem=rka,
+            device_id={"sub": sxy * 8 + z},
+            device_id_type=MESH,
+        ).start()
+        return 0
+
+    lax.fori_loop(0, 3, go_k, 0)
+    weights = []
+    for _ in range(4):
+        tiles = back_step(tiles)
+        weights.append(tiles[REACH])
+    weights = jnp.concatenate(weights, axis=0)
+    seen = seen + seen_flows(weights)
+    reduce_a(1, draws_of(seen, 7))
+
     sacc[...] = jnp.zeros((256, LANES), F32)
-    whole(recv1.at[pl.ds(0, PEERS)], s1, r1).wait_recv()
+    whole(recv1.at[pl.ds(0, PEERS), pl.ds(0, 2 * REACH)], s1, r1).wait_recv()
     lane_e = iota((PAIR, 128), 1) - (INTERFACE - 128)
     for a in range(SLAB):
         arrived = recv1[:, a].reshape(2 * SUBS, LANES)
@@ -252,10 +387,9 @@
         zb[top : top + PAIR, 128:LANES] = high.astype(BF16)
     sacc[32:224] = zf[224:416]
     usum[...] = jnp.zeros((PAIR, LANES), F32)
-    flow_map = mp.at[side]
 
     def half(i):
-        u = dot(L2[i], zb[192 * i : 192 * i + 256])
+        u = dot(L2[i, 32:224], zb[192 * i : 192 * i + 256])
         if i == 1:
             usum[...] += u[32:160]
         return u.astype(BF16)
@@ -277,74 +411,13 @@
         step()
         return carry
 
-    def own_part(with_lanes):
-        marked = zb[OWN : OWN + PAIR, INTERFACE : INTERFACE + RES]
-        return dot_ta(marked, with_lanes)
-
-    def to_z(buf, t, send_sem, recv_sem):
-        for z in ring:
-            pltpu.make_async_remote_copy(
-                src_ref=buf.at[t, sz],
-                dst_ref=buf.at[t, sz],
-                send_sem=send_sem.at[t],
-                recv_sem=recv_sem.at[t],
-                device_id={"sub": sxy * 8 + z},
-                device_id_type=MESH,
-            ).start()
-
-    def start_b(t):
-        here_b = dist * 8 + sxy
-        for at in level:
-            for k in (2, 1, 3, 0):
-                if k == 0 and at is level[-1]:
-                    continue
-                pltpu.make_async_remote_copy(
-                    src_ref=arb.at[t, here_b],
-                    dst_ref=arb.at[t, here_b],
-                    send_sem=sb.at[t],
-                    recv_sem=rb.at[t],
-                    device_id={"district": dist_at[k], "sub": at + sz},
-                    device_id_type=MESH,
-                ).start()
-
-    def all_of(buf, t, count, send_sem, recv_sem):
-        return whole(buf.at[t, pl.ds(0, count)], send_sem.at[t], recv_sem.at[t])
-
-    def reduce_a(t, part):
-        ara[t, sz] = folded(part)
-        to_z(ara, t, sa, ra)
-
-    def reduce_b(t):
-        all_of(ara, t, 7, sa, ra).wait_recv()
-        arb[t, dist * 8 + sxy] = jnp.sum(ara[t], axis=0)
-        start_b(t)
-
-    def reduce_end(t):
-        all_of(arb, t, 31, sb, rb).wait_recv()
-        return unfolded(jnp.sum(arb[t], axis=0))
-
     lax.fori_loop(0, 3, full_step, 0)
-    reduce_a(0, own_part(zb[OWN : OWN + PAIR, 0:128]))
     marks = zb[OWN : OWN + PAIR, INTERFACE:LANES]
-    aka[0, sz // 2] = folded(own_part(marks))
-
-    def go_k(k, _):
-        z = lax.rem(sz + 2 + 2 * k, 8)
-        pltpu.make_async_remote_copy(
-            src_ref=aka.at[0, sz // 2],
-            dst_ref=aka.at[0, sz // 2],
-            send_sem=ska,
-            recv_sem=rka,
-            device_id={"sub": sxy * 8 + z},
-            device_id_type=MESH,
-        ).start()
-        return 0
-
-    lax.fori_loop(0, 3, go_k, 0)
     near_marks = dot(lown[...], zb[192:448])[:, INTERFACE:LANES].astype(BF16)
     step()
     step()
     step()
+    reduce_b(0)
 
     u = half(1)
     prices = (STEP * usum[...]).astype(BF16)
@@ -363,10 +436,8 @@
     recv2[sub] = send2[slot_of(sub)]
 
     advance(1, u)
-    reduce_a(1, own_part(zb[OWN : OWN + PAIR, 0:128]))
     price0 = dot(lown[...], sacc[...].astype(BF16))[:, 0:INTERFACE]
 
-    reduce_b(0)
     whole(aka.at[0, pl.ds(0, 3)], ska, rka).wait_recv()
     akb[0, sxy] = jnp.sum(aka[0], axis=0)
 
@@ -397,21 +468,19 @@
     def powers_of(m_ref, count):
         powers = [wide]
         for _ in range(count):
-            powers.append(
-                dot(powers[-1].astype(BF16), m_ref[0:INTERFACE, 0:INTERFACE]) * (-1.0 / STEP)
-            )
+            powers.append(dot2(powers[-1], m_ref[0:INTERFACE, 0:INTERFACE]) * (-1.0 / STEP))
         return powers
 
-    def stack(powers, weights):
-        return jnp.concatenate(
-            [p * (w / b) for p, w, b in zip(powers, weights, binom)], axis=0
-        ).astype(BF16)
+    def stack(powers, weights, counts=binom):
+        return jnp.concatenate([p * (w / b) for p, w, b in zip(powers, weights, counts)], axis=0)
 
     powers = powers_of(flow_map, 4)
     whole(akb.at[0, pl.ds(0, 7)], skb, rkb).wait_recv()
-    unit = unfolded(jnp.sum(akb[0], axis=0)).astype(BF16)
+    unit = unfolded(jnp.sum(akb[0], axis=0))
     here_c = dist * 2 + side
-    arc[here_c] = folded(dot(unit, stack(powers[1:], in_flow))[:, 0:128])
+    caused = two_parts(stack(powers[1:], in_flow, (1.0,) * 4))
+    caused = dot2(unit, caused[0:BLOCK]) + dot(unit.astype(BF16), caused[BLOCK:PAIR])
+    arc[here_c] = folded(caused[:, 0:128])
 
     def go_c(k, _):
         there = lax.rem(here_c + k, 8)
@@ -426,7 +495,7 @@
         return 0
 
     lax.fori_loop(1, 8, go_c, 0)
-    final_price = STEP * (price0 + dot(near_marks, stack(powers[1:], in_sum)))
+    final_price = STEP * (price0 + dot(near_marks, stack(powers[1:], in_sum).astype(BF16)))
     halves = [final_price[0:BLOCK], final_price[BLOCK:PAIR]]
     price_s[...] = jnp.where(side == 0, halves[1], halves[0])
     price_copy = pltpu.make_async_remote_copy(
@@ -441,7 +510,7 @@
     price_o[side] = jnp.where(side == 0, halves[0], halves[1])
     for d in range(2):
         powers_d = powers_of(mp.at[d], 3)
-        vfull[d, INTERFACE:LANES] = dot(stack(powers_d, in_price), cts[d]).astype(BF16)
+        vfull[d, INTERFACE:LANES] = dot(stack(powers_d, in_price).astype(BF16), cts[d]).astype(BF16)
 
     whole(recv2.at[pl.ds(0, PEERS)], s2, r2).wait_recv()
     mine = dot(p5[...], recv2[...].reshape(2 * SUBS, LANES)).astype(BF16)
@@ -457,7 +526,7 @@
     dual_o[...] = duals + (draws0 + draws1 - capacity) * scale
 
     whole(mbuf.at[pl.ds(0, 2 * SLAB - 1)], sm, rm).wait_send()
-    whole(recv1.at[pl.ds(0, PEERS)], s1, r1).wait_send()
+    whole(recv1.at[pl.ds(0, PEERS), pl.ds(0, 2 * REACH)], s1, r1).wait_send()
     whole(recv2.at[pl.ds(0, PEERS)], s2, r2).wait_send()
     for t in range(2):
         all_of(ara, t, 7, sa, ra).wait_send()
@@ -465,6 +534,7 @@
     whole(aka.at[0, pl.ds(0, 3)], ska, rka).wait_send()
     whole(akb.at[0, pl.ds(0, 7)], skb, rkb).wait_send()
     whole(arc.at[pl.ds(0, 7)], sc, rc).wait_send()
+    whole(recv1.at[pl.ds(0, PEERS), REACH], se, re).wait_send()
     price_copy.wait_send()
 
 
@@ -503,15 +573,15 @@
             pltpu.VMEM((2, 4, BLOCK), jnp.int32),
             pltpu.VMEM((2, BLOCK), jnp.int32),
             pltpu.VMEM((RES, HORIZON), F32),
-            pltpu.VMEM((16, 128), BF16),
+            pltpu.VMEM((2, 16, 128), BF16),
             pltpu.VMEM((2, INTERFACE, UNKNOWNS), BF16),
             pltpu.VMEM((2, PAIRS + 2 * REACH, 2, LANES), BF16),
             pltpu.VMEM((SUBS, SLAB, 2, LANES), BF16),
             pltpu.VMEM((SUBS, 2, LANES), BF16),
             pltpu.VMEM((SUBS, 2, LANES), BF16),
             pltpu.VMEM((2 * SLAB, 16, 128), BF16),
-            pltpu.VMEM((ROWS, 8), F32),
-            pltpu.VMEM((3, 192, 256), BF16),
+            pltpu.VMEM((ROWS, 16), F32),
+            pltpu.VMEM((3, 256, 256), BF16),
             pltpu.VMEM((PAIR, 256), BF16),
             pltpu.VMEM((128, 128), BF16),
             pltpu.VMEM((128, 128), BF16),
@@ -530,7 +600,7 @@
             dma((10,)),
             dma, dma, dma, dma, dma, dma, dma, dma,
             dma((2,)), dma((2,)), dma((2,)), dma((2,)),
-            dma, dma, dma, dma, dma, dma,
+            dma, dma, dma, dma, dma, dma, dma, dma,
         ],
         compiler_params=pltpu.CompilerParams(
             collective_id=0, has_side_effects=True, vmem_limit_bytes=VMEM_LIMIT

time: 41.6 us -> 38.5 us (0.925)
  Pallas kernels: 40.8 us -> 37.7 us
    pallas_call x1, Pallas kernels: 40 us -> 36.9 us  [on_device(): pl.pallas_call(kernel, out_shape=(pltpu.VMEM((2, BLOCK, UNKNOWNS), F32),...]
where the time goes in v4:
time: 38.5 us; the launch traced here: 38.4 us
  Pallas kernels  37.7 us (98%)
  between operations  0.64 us (2%)
    pallas_call x1, Pallas kernels, on_device(): pl.pallas_call(kernel, out_shape=(pltpu.VMEM((2, BLOCK, UNKNOWNS), F32),...  36.9 us
    pallas_call x1, Pallas kernels, on_device(): pl.pallas_call(write_out, out_shape=(jax.ShapeDtypeStruct((2, BLOCK, UNKN...  0.82 us

profile of v4, /device:TPU:1, one launch (start us, length us, event | category | flops | bytes accessed | tf_op | source)
XLA Modules:
  0.0 38.4 jit_solution(3425843435063841210)
XLA Ops:
  0.6 36.9 %shard_map.94 = (f32[2,64,768]{2,1,0:T(8,128)S(1)}, f32[2,64,192]{2,1,0:T(8,128)S(1)}, f32[16,48]{1,0:T(8,128)S(1)}) custom-call(bf16[2,64,768]{2,1,0:T(8,128)(2,1)} %cost.1, bf16[2,192,768]{2,1,0:T(8,128)(2,1)} %bitcast.5, bf16[2,768,768]{2,1,0:T(8,128)(2,1)} %solve.1, s32[32,2,128]{2,1,0:T(2,128)} %bitcast.6, s32[2,4,64]{2,1,0:T(4,128)} %bitcast.7, ...), custom_call_target="tpu_custom_call" | custom-call | tf_op jit(solution)/shard_map/pallas_call | solution.py:557
  37.5 0.8 %shard_map.95 = (f32[2,64,768]{2,1,0:T(8,128)}, f32[2,64,192]{2,1,0:T(8,128)}, f32[16,48]{1,0:T(8,128)}) custom-call(f32[2,64,768]{2,1,0:T(8,128)S(1)} %get-tuple-element.6.plan, f32[2,64,192]{2,1,0:T(8,128)S(1)} %get-tuple-element.7.price, f32[16,48]{1,0:T(8,128)S(1)} %get-tuple-element.8.dual), custom_call_target="tpu_custom_call" | custom-call | tf_op jit(solution)/shard_map/pallas_call | solution.py:612

commit v5 on v4

--- a/solution.py
+++ b/solution.py
@@ -20,7 +20,7 @@
 LANES = 256
 STEP = 0.3
 PEERS = SUBS - 1
-OTHERS = 27
+OTHERS = 24
 VMEM_LIMIT = 67043328 - 700 * 1024
 
 
@@ -71,9 +71,9 @@
     cost, coup, solve, rel_h, near_h, owner_h, cap_h,
     plan_o, price_o, dual_o,
     X, S, C, cs, vfull, rel, near_in, owner_in, cap, meta, cts, send1, recv1, send2, recv2,
-    mbuf, offs, L2, lown, p4t, p5, mp, zf, zb, sacc, usum, ara, arb, aka, akb, arc, price_s, price_r,
-
-    load_sem, s1, r1, s2, r2, sm, rm, sp, rp, sa, ra, sb, rb, ska, rka, skb, rkb, sc, rc, se, re,
+    mbuf, offs, L2, lown, p4t, p5, mp, zf, zb, sacc, usum, ara, arb, aka, akb, akc, maps, price_s, price_r,
+
+    load_sem, s1, r1, s2, r2, sm, rm, sp, rp, sa, ra, sb, rb, ska, rka, skb, rkb, sc, rc, se, re, skc, rkc,
 ):
     sub = lax.axis_index("sub")
     dist = lax.axis_index("district")
@@ -114,8 +114,6 @@
     for at in level:
         for k in range(1, DISTS):
             hello({"district": dist_at[k], "sub": at + sz})
-    for k in range(1, DISTS):
-        hello({"district": dist_at[k], "sub": 2 * pair + 1 - side})
 
     def whole(buf, send_sem, recv_sem):
         return pltpu.make_async_remote_copy(
@@ -218,6 +216,18 @@
         shift = jnp.where(li - (INTERFACE - 128) == ri + RES, 1.0, 0.0)
         mp[d, INTERFACE:LANES, 128:LANES] = shift.astype(BF16)
         vfull[d, 0:INTERFACE] = cts_d
+    for d in range(2):
+        wide_map = mp[d, 0:INTERFACE, 0:INTERFACE]
+        size = jnp.max(
+            jnp.sum(jnp.abs(wide_map.astype(F32)), axis=0, keepdims=True), axis=1, keepdims=True
+        )
+        size = (1.0 + 1.02 * size).astype(BF16).astype(F32)
+        small_map, tiles = wide_map[0:HORIZON].astype(F32) / size, []
+        for j in range(4):
+            if j:
+                small_map = dot2(small_map, wide_map) / size
+            tiles += [small_map[:, 0:HORIZON], jnp.broadcast_to(size, (HORIZON, BLOCK - HORIZON))]
+        maps[dist, d] = jnp.concatenate(tiles, axis=1).astype(BF16)
 
     by_pair = rel[...].reshape(SUBS, PAIR)
     si, sj = iota((SUBS, SUBS), 0), iota((SUBS, SUBS), 1)
@@ -258,28 +268,29 @@
         if i == 1:
             lown[...] = near[64:192]
 
-    def to_z(buf, t, send_sem, recv_sem):
+    def to_z(buf, send_sem, recv_sem):
         for z in ring:
             pltpu.make_async_remote_copy(
-                src_ref=buf.at[t, sz],
-                dst_ref=buf.at[t, sz],
-                send_sem=send_sem.at[t],
-                recv_sem=recv_sem.at[t],
+                src_ref=buf.at[sz],
+                dst_ref=buf.at[sz],
+                send_sem=send_sem,
+                recv_sem=recv_sem,
                 device_id={"sub": sxy * 8 + z},
                 device_id_type=MESH,
             ).start()
 
-    def start_b(t):
-        here_b = dist * 8 + sxy
+    here_b = dist * 8 + sxy
+
+    def start_b(buf, send_sem, recv_sem):
         for at in level:
             for k in (2, 1, 3, 0):
                 if k == 0 and at is level[-1]:
                     continue
                 pltpu.make_async_remote_copy(
-                    src_ref=arb.at[t, here_b],
-                    dst_ref=arb.at[t, here_b],
-                    send_sem=sb.at[t],
-                    recv_sem=rb.at[t],
+                    src_ref=buf.at[here_b],
+                    dst_ref=buf.at[here_b],
+                    send_sem=send_sem,
+                    recv_sem=recv_sem,
                     device_id={"district": dist_at[k], "sub": at + sz},
                     device_id_type=MESH,
                 ).start()
@@ -289,16 +300,16 @@
 
     def reduce_a(t, part):
         ara[t, sz] = folded(part)
-        to_z(ara, t, sa, ra)
+        to_z(ara.at[t], sa.at[t], ra.at[t])
 
     def reduce_b(t):
         all_of(ara, t, 7, sa, ra).wait_recv()
-        arb[t, dist * 8 + sxy] = jnp.sum(ara[t], axis=0)
-        start_b(t)
+        arb[t, here_b] = jnp.sum(ara[t], axis=0).astype(BF16)
+        start_b(arb.at[t], sb.at[t], rb.at[t])
 
     def reduce_end(t):
         all_of(arb, t, 31, sb, rb).wait_recv()
-        return unfolded(jnp.sum(arb[t], axis=0))
+        return unfolded(jnp.sum(arb[t].astype(F32), axis=0))
 
     flow_map = mp.at[side]
     owners = []
@@ -330,11 +341,14 @@
         sums = sums[0:BLOCK] + sums[BLOCK : 2 * BLOCK]
         return [sums[RES * j : RES * (j + 1)] for j in range(4)]
 
+    def next_power(total, seen, count, j):
+        total = dot2(total, flow_map[0:INTERFACE, 0:INTERFACE])
+        return total + seen[j] * float(math.comb(count, j))
+
     def draws_of(seen, count):
         total = seen[count]
         for j in reversed(range(count)):
-            total = dot2(total, flow_map[0:INTERFACE, 0:INTERFACE])
-            total = total + seen[j] * float(math.comb(count, j))
+            total = next_power(total, seen, count, j)
         return total[:, 0:128]
 
     weights, tiles = [own_owners], owners
@@ -342,27 +356,15 @@
         tiles = back_step(tiles)
         weights.append(tiles[REACH])
     weights = jnp.concatenate(weights, axis=0)
+    whole(recv1.at[pl.ds(0, PEERS), REACH], se, re).wait_recv()
+    seen = seen_flows(weights)
     unit = dot_tb(two_parts(weights), own_owners.astype(BF16))
     unit = unit[0:BLOCK] + unit[BLOCK : 2 * BLOCK]
     unit = [unit[RES * j : RES * (j + 1), 0:RES] for j in range(4)]
-    aka[0, sz // 2] = folded(jnp.concatenate(unit, axis=1))
-    whole(recv1.at[pl.ds(0, PEERS), REACH], se, re).wait_recv()
-    seen = seen_flows(weights)
-    reduce_a(0, draws_of(seen, 3))
-
-    def go_k(k, _):
-        z = lax.rem(sz + 2 + 2 * k, 8)
-        pltpu.make_async_remote_copy(
-            src_ref=aka.at[0, sz // 2],
-            dst_ref=aka.at[0, sz // 2],
-            send_sem=ska,
-            recv_sem=rka,
-            device_id={"sub": sxy * 8 + z},
-            device_id_type=MESH,
-        ).start()
-        return 0
-
-    lax.fori_loop(0, 3, go_k, 0)
+    early = draws_of(seen, 3)
+    reduce_a(0, early)
+    aka[sz] = folded(jnp.concatenate(unit, axis=1))
+    to_z(aka, ska, rka)
     weights = []
     for _ in range(4):
         tiles = back_step(tiles)
@@ -373,6 +375,15 @@
 
     sacc[...] = jnp.zeros((256, LANES), F32)
     whole(recv1.at[pl.ds(0, PEERS), pl.ds(0, 2 * REACH)], s1, r1).wait_recv()
+    for k in (2, 1, 3):
+        pltpu.make_async_remote_copy(
+            src_ref=maps.at[dist],
+            dst_ref=maps.at[dist],
+            send_sem=sc,
+            recv_sem=rc,
+            device_id={"district": dist_at[k]},
+            device_id_type=MESH,
+        ).start()
     lane_e = iota((PAIR, 128), 1) - (INTERFACE - 128)
     for a in range(SLAB):
         arrived = recv1[:, a].reshape(2 * SUBS, LANES)
@@ -407,20 +418,25 @@
         for i, u in enumerate(us):
             advance(i, u)
 
-    def full_step(_, carry):
+    for k in range(6):
         step()
-        return carry
-
-    lax.fori_loop(0, 3, full_step, 0)
-    marks = zb[OWN : OWN + PAIR, INTERFACE:LANES]
-    near_marks = dot(lown[...], zb[192:448])[:, INTERFACE:LANES].astype(BF16)
-    step()
-    step()
-    step()
     reduce_b(0)
+    whole(aka.at[pl.ds(0, 7)], ska, rka).wait_recv()
+    by_side = [aka[d] + aka[d + 2] + aka[d + 4] + aka[d + 6] for d in range(2)]
+    akb[sxy] = jnp.concatenate(by_side, axis=0)
+    for at in level[:-1]:
+        pltpu.make_async_remote_copy(
+            src_ref=akb.at[sxy],
+            dst_ref=akb.at[sxy],
+            send_sem=skb,
+            recv_sem=rkb,
+            device_id={"sub": at + sz},
+            device_id_type=MESH,
+        ).start()
 
     u = half(1)
     prices = (STEP * usum[...]).astype(BF16)
+    marks = zb[OWN : OWN + PAIR, INTERFACE:LANES]
     back = jnp.concatenate([prices[:, 0:INTERFACE], marks], axis=1)
     send2[...] = dot(p4t[...], back).astype(BF16).reshape(SUBS, 2, LANES)
 
@@ -435,69 +451,13 @@
         ).start()
     recv2[sub] = send2[slot_of(sub)]
 
+    near_marks = dot(lown[...], zb[192:448, 128:LANES])[:, INTERFACE - 128 :]
     advance(1, u)
-    price0 = dot(lown[...], sacc[...].astype(BF16))[:, 0:INTERFACE]
-
-    whole(aka.at[0, pl.ds(0, 3)], ska, rka).wait_recv()
-    akb[0, sxy] = jnp.sum(aka[0], axis=0)
-
-    def go_kb(k, _):
-        xy = lax.rem(sxy + k, 8)
-        pltpu.make_async_remote_copy(
-            src_ref=akb.at[0, sxy],
-            dst_ref=akb.at[0, sxy],
-            send_sem=skb,
-            recv_sem=rkb,
-            device_id={"sub": xy * 8 + sz},
-            device_id_type=MESH,
-        ).start()
-        return 0
-
-    lax.fori_loop(1, 8, go_kb, 0)
-    reduce_b(1)
-    capacity = cap[...]
-    scale = 1.0 / math.sqrt(DISTS * 2 * SUBS * BLOCK / (2 * RES))
-    duals = (reduce_end(0)[:, 0:HORIZON] - capacity) * scale
-    wide = jnp.concatenate([duals, jnp.zeros((RES, INTERFACE - HORIZON), F32)], axis=1)
-
-    binom = (1.0, 3.0, 3.0, 1.0)
-    in_price = (1.0, -0.9, 0.27, -0.027)
-    in_flow = (-1.0, 0.9, -0.27, 0.027)
-    in_sum = (-4.0, 1.8, -0.36, 0.027)
-
-    def powers_of(m_ref, count):
-        powers = [wide]
-        for _ in range(count):
-            powers.append(dot2(powers[-1], m_ref[0:INTERFACE, 0:INTERFACE]) * (-1.0 / STEP))
-        return powers
-
-    def stack(powers, weights, counts=binom):
-        return jnp.concatenate([p * (w / b) for p, w, b in zip(powers, weights, counts)], axis=0)
-
-    powers = powers_of(flow_map, 4)
-    whole(akb.at[0, pl.ds(0, 7)], skb, rkb).wait_recv()
-    unit = unfolded(jnp.sum(akb[0], axis=0))
-    here_c = dist * 2 + side
-    caused = two_parts(stack(powers[1:], in_flow, (1.0,) * 4))
-    caused = dot2(unit, caused[0:BLOCK]) + dot(unit.astype(BF16), caused[BLOCK:PAIR])
-    arc[here_c] = folded(caused[:, 0:128])
-
-    def go_c(k, _):
-        there = lax.rem(here_c + k, 8)
-        pltpu.make_async_remote_copy(
-            src_ref=arc.at[here_c],
-            dst_ref=arc.at[here_c],
-            send_sem=sc,
-            recv_sem=rc,
-            device_id={"district": there // 2, "sub": 2 * pair + lax.rem(there, 2)},
-            device_id_type=MESH,
-        ).start()
-        return 0
-
-    lax.fori_loop(1, 8, go_c, 0)
-    final_price = STEP * (price0 + dot(near_marks, stack(powers[1:], in_sum).astype(BF16)))
-    halves = [final_price[0:BLOCK], final_price[BLOCK:PAIR]]
-    price_s[...] = jnp.where(side == 0, halves[1], halves[0])
+    near_sums = dot(lown[...], sacc[...].astype(BF16))[:, 0:INTERFACE]
+    prices = jnp.concatenate([near_sums, near_marks], axis=1)
+    kept = jnp.where(side == 0, prices[0:BLOCK], prices[BLOCK:PAIR])
+    price0, marks0 = kept[:, 0:INTERFACE], kept[:, INTERFACE:LANES]
+    price_s[...] = jnp.where(side == 0, prices[BLOCK:PAIR], prices[0:BLOCK])
     price_copy = pltpu.make_async_remote_copy(
         src_ref=price_s,
         dst_ref=price_r,
@@ -507,10 +467,50 @@
         device_id_type=MESH,
     )
     price_copy.start()
-    price_o[side] = jnp.where(side == 0, halves[0], halves[1])
-    for d in range(2):
-        powers_d = powers_of(mp.at[d], 3)
-        vfull[d, INTERFACE:LANES] = dot(stack(powers_d, in_price).astype(BF16), cts[d]).astype(BF16)
+
+    reduce_b(1)
+    whole(akb.at[pl.ds(0, 7)], skb, rkb).wait_recv()
+    akc[dist] = jnp.sum(akb[...], axis=0)
+    for k in (2, 1, 3):
+        pltpu.make_async_remote_copy(
+            src_ref=akc.at[dist],
+            dst_ref=akc.at[dist],
+            send_sem=skc,
+            recv_sem=rkc,
+            device_id={"district": dist_at[k]},
+            device_id_type=MESH,
+        ).start()
+    capacity = cap[...]
+    scale = 1.0 / math.sqrt(DISTS * 2 * SUBS * BLOCK / (2 * RES))
+    duals = (reduce_end(0)[:, 0:HORIZON] - capacity) * scale
+    wide = jnp.concatenate([duals, jnp.zeros((RES, INTERFACE - HORIZON), F32)], axis=1)
+
+    binom = (1.0, 6.0, 15.0, 20.0)
+    in_price = (1.0, -0.9, 0.27, -0.027)
+    in_sum = (-4.0, 1.8, -0.36, 0.027)
+
+    def powers_of(m_ref, count):
+        powers = [wide]
+        for _ in range(count):
+            powers.append(dot2(powers[-1], m_ref[0:INTERFACE, 0:INTERFACE]) * (-1.0 / STEP))
+        return powers
+
+    def stack(powers, weights):
+        parts = [p * (w / b) for p, w, b in zip(powers, weights, binom)]
+        return jnp.concatenate(parts, axis=0).astype(BF16)
+
+    powers_by = [powers_of(mp.at[d], 4) for d in range(2)]
+    sums = [stack(powers_by[d][1:], in_sum) for d in range(2)]
+    here_sums = jnp.where(side == 0, sums[0], sums[1])
+    there_sums = jnp.where(side == 0, sums[1], sums[0])
+    price_o[side] = STEP * (price0 + dot(marks0.astype(BF16), here_sums))
+    price_copy.wait_recv()
+    sent = price_r[...]
+    price_o[1 - side] = STEP * (
+        sent[:, 0:INTERFACE] + dot(sent[:, INTERFACE:LANES].astype(BF16), there_sums)
+    )
+    for d in range(2):
+        vfull[d, INTERFACE:LANES] = dot(stack(powers_by[d][0:4], in_price), cts[d]).astype(BF16)
 
     whole(recv2.at[pl.ds(0, PEERS)], s2, r2).wait_recv()
     mine = dot(p5[...], recv2[...].reshape(2 * SUBS, LANES)).astype(BF16)
@@ -518,11 +518,26 @@
         at = d * BLOCK
         plan_o[d] = -(cs[at : at + BLOCK] + dot(mine[at : at + BLOCK], vfull[d]))
 
-    price_copy.wait_recv()
-    price_o[1 - side] = price_r[...]
+    whole(akc.at[pl.ds(0, 3)], skc, rkc).wait_recv()
+    whole(maps.at[pl.ds(0, 3)], sc, rc).wait_recv()
+    units, causes = [], []
+    for k in range(DISTS):
+        unit = akc[k]
+        for d in range(2):
+            units.append(unfolded(unit[8 * d : 8 * d + 8]))
+            size = maps[k, d, 0:1, HORIZON : HORIZON + 1].astype(F32)
+            moved = dot2(duals, maps[k, d])
+            for j in range(4):
+                part = moved[:, BLOCK * j : BLOCK * (j + 1)] * (math.comb(3, j) / STEP)
+                for _ in range(j + 1):
+                    part = part * size
+                causes.append(part)
+    units, causes = jnp.concatenate(units, axis=1), two_parts(jnp.concatenate(causes, axis=0))
+    count = units.shape[1]
+    draws1 = dot2(units, causes[0:count]) + dot(units.astype(BF16), causes[count : 2 * count])
+    draws1 = draws1[:, 0:HORIZON]
+
     draws0 = reduce_end(1)[:, 0:HORIZON]
-    whole(arc.at[pl.ds(0, 7)], sc, rc).wait_recv()
-    draws1 = unfolded(jnp.sum(arc[...], axis=0))[:, 0:HORIZON]
     dual_o[...] = duals + (draws0 + draws1 - capacity) * scale
 
     whole(mbuf.at[pl.ds(0, 2 * SLAB - 1)], sm, rm).wait_send()
@@ -531,9 +546,10 @@
     for t in range(2):
         all_of(ara, t, 7, sa, ra).wait_send()
         all_of(arb, t, 31, sb, rb).wait_send()
-    whole(aka.at[0, pl.ds(0, 3)], ska, rka).wait_send()
-    whole(akb.at[0, pl.ds(0, 7)], skb, rkb).wait_send()
-    whole(arc.at[pl.ds(0, 7)], sc, rc).wait_send()
+    whole(aka.at[pl.ds(0, 7)], ska, rka).wait_send()
+    whole(akb.at[pl.ds(0, 7)], skb, rkb).wait_send()
+    whole(akc.at[pl.ds(0, 3)], skc, rkc).wait_send()
+    whole(maps.at[pl.ds(0, 3)], sc, rc).wait_send()
     whole(recv1.at[pl.ds(0, PEERS), REACH], se, re).wait_send()
     price_copy.wait_send()
 
@@ -591,16 +607,17 @@
             pltpu.VMEM((256, LANES), F32),
             pltpu.VMEM((PAIR, LANES), F32),
             pltpu.VMEM((2, 8, 8, 128), F32),
-            pltpu.VMEM((2, 32, 8, 128), F32),
-            pltpu.VMEM((1, 4, 8, 128), F32),
-            pltpu.VMEM((1, 8, 8, 128), F32),
+            pltpu.VMEM((2, 32, 8, 128), BF16),
             pltpu.VMEM((8, 8, 128), F32),
-            pltpu.VMEM((BLOCK, INTERFACE), F32),
-            pltpu.VMEM((BLOCK, INTERFACE), F32),
+            pltpu.VMEM((8, 16, 128), F32),
+            pltpu.VMEM((DISTS, 16, 128), F32),
+            pltpu.VMEM((DISTS, 2, HORIZON, LANES), BF16),
+            pltpu.VMEM((BLOCK, LANES), F32),
+            pltpu.VMEM((BLOCK, LANES), F32),
             dma((10,)),
             dma, dma, dma, dma, dma, dma, dma, dma,
             dma((2,)), dma((2,)), dma((2,)), dma((2,)),
-            dma, dma, dma, dma, dma, dma, dma, dma,
+            dma, dma, dma, dma, dma, dma, dma, dma, dma, dma,
         ],
         compiler_params=pltpu.CompilerParams(
             collective_id=0, has_side_effects=True, vmem_limit_bytes=VMEM_LIMIT

time: 38.5 us -> 38 us (0.987)
  Pallas kernels: 37.7 us -> 37.2 us
    pallas_call x1, Pallas kernels: 36.9 us -> 36.4 us  [on_device(): pl.pallas_call(kernel, out_shape=(pltpu.VMEM((2, BLOCK, UNKNOWNS), F32),...]
where the time goes in v5:
time: 38 us; the launch traced here: 37.9 us
  Pallas kernels  37.2 us (98%)
  between operations  0.64 us (2%)
    pallas_call x1, Pallas kernels, on_device(): pl.pallas_call(kernel, out_shape=(pltpu.VMEM((2, BLOCK, UNKNOWNS), F32),...  36.4 us
    pallas_call x1, Pallas kernels, on_device(): pl.pallas_call(write_out, out_shape=(jax.ShapeDtypeStruct((2, BLOCK, UNKN...  0.82 us

profile of v5, /device:TPU:1, one launch (start us, length us, event | category | flops | bytes accessed | tf_op | source)
XLA Modules:
  0.0 37.9 jit_solution(6544573729643560489)
XLA Ops:
  0.6 36.4 %shard_map.94 = (f32[2,64,768]{2,1,0:T(8,128)S(1)}, f32[2,64,192]{2,1,0:T(8,128)S(1)}, f32[16,48]{1,0:T(8,128)S(1)}) custom-call(bf16[2,64,768]{2,1,0:T(8,128)(2,1)} %cost.1, bf16[2,192,768]{2,1,0:T(8,128)(2,1)} %bitcast.5, bf16[2,768,768]{2,1,0:T(8,128)(2,1)} %solve.1, s32[32,2,128]{2,1,0:T(2,128)} %bitcast.6, s32[2,4,64]{2,1,0:T(4,128)} %bitcast.7, ...), custom_call_target="tpu_custom_call" | custom-call | tf_op jit(solution)/shard_map/pallas_call | solution.py:573
  37.1 0.8 %shard_map.95 = (f32[2,64,768]{2,1,0:T(8,128)}, f32[2,64,192]{2,1,0:T(8,128)}, f32[16,48]{1,0:T(8,128)}) custom-call(f32[2,64,768]{2,1,0:T(8,128)S(1)} %get-tuple-element.6.plan, f32[2,64,192]{2,1,0:T(8,128)S(1)} %get-tuple-element.7.price, f32[16,48]{1,0:T(8,128)S(1)} %get-tuple-element.8.dual), custom_call_target="tpu_custom_call" | custom-call | tf_op jit(solution)/shard_map/pallas_call | solution.py:629

commit v6 on v5

--- a/solution.py
+++ b/solution.py
@@ -14,6 +14,7 @@
 PAIRS = SUBS // 2
 REACH = 2
 SLAB = 2 * REACH + 1
+SPAN = PAIRS + 2 * REACH
 PAIR = 2 * BLOCK
 ROWS = SLAB * PAIR
 OWN = REACH * PAIR
@@ -70,7 +71,7 @@
 def kernel(
     cost, coup, solve, rel_h, near_h, owner_h, cap_h,
     plan_o, price_o, dual_o,
-    X, S, C, cs, vfull, rel, near_in, owner_in, cap, meta, cts, send1, recv1, send2, recv2,
+    X, S, C, cs, vfull, rel, near_in, owner_in, cap, meta, cts, send1, recv1, sendh, recvh, send2, recv2,
     mbuf, offs, L2, lown, p4t, p5, mp, zf, zb, sacc, usum, ara, arb, aka, akb, akc, maps, price_s, price_r,
 
     load_sem, s1, r1, s2, r2, sm, rm, sp, rp, sa, ra, sb, rb, ska, rka, skb, rkb, sc, rc, se, re, skc, rkc,
@@ -148,15 +149,19 @@
     first = jnp.concatenate([first, jnp.zeros((2 * BLOCK, LANES - INTERFACE), BF16)], axis=1)
     lane = iota((2 * BLOCK, 2 * BLOCK), 1)
     row = iota((2 * BLOCK, 2 * BLOCK), 0)
-    to_dest = jnp.where(own_block + BLOCK * (lane // BLOCK) == row, 1.0, 0.0).astype(BF16)
     eye = jnp.where(lane == row, 1.0, 0.0).astype(BF16)
-    sorted_rows = dot(to_dest, first).astype(BF16)
-    for d in range(2):
-        send1[d, 0:REACH] = jnp.zeros((REACH, 2, LANES), BF16)
-        send1[d, REACH + PAIRS : PAIRS + 2 * REACH] = jnp.zeros((REACH, 2, LANES), BF16)
-        send1[d, REACH : REACH + PAIRS] = sorted_rows[d * BLOCK : (d + 1) * BLOCK].reshape(
-            PAIRS, 2, LANES
-        )
+    dest = own_block + 2 * SPAN * (lane[0:1] // BLOCK)
+    at_row = iota((4 * SPAN, 2 * BLOCK), 0)
+    sorted_rows, next_rows = [
+        dot(jnp.where(dest + 2 * skip == at_row, 1.0, 0.0).astype(BF16), first).astype(BF16)
+        for skip in (REACH, REACH - 1)
+    ]
+    send1[...] = sorted_rows.reshape(2 * SPAN, 2, LANES)
+    rest = [t[:, 128:INTERFACE] for t in (sorted_rows, next_rows)]
+    for k, tile in enumerate(
+        (sorted_rows[:, 0:128], next_rows[:, 0:128], jnp.concatenate(rest, axis=1))
+    ):
+        sendh[:, k] = tile.reshape(2 * SPAN, 2, 128)
 
     pl.semaphore_wait(barrier, PEERS + OTHERS)
 
@@ -184,24 +189,27 @@
     slot = slot_of(sub)
     for peer in peers:
         pltpu.make_async_remote_copy(
-            src_ref=send1.at[lax.rem(peer, 2), REACH + peer // 2],
-            dst_ref=recv1.at[slot, REACH],
+            src_ref=send1.at[SPAN * lax.rem(peer, 2) + peer // 2 + REACH],
+            dst_ref=recv1.at[slot],
             send_sem=se,
             recv_sem=re,
             device_id={"sub": peer},
             device_id_type=MESH,
         ).start()
     for peer in peers:
-        for first in (0, REACH + 1):
+        for k in range(2):
             pltpu.make_async_remote_copy(
-                src_ref=send1.at[lax.rem(peer, 2), pl.ds(peer // 2 + first, REACH)],
-                dst_ref=recv1.at[slot, pl.ds(first, REACH)],
+                src_ref=sendh.at[SPAN * lax.rem(peer, 2) + peer // 2 + (REACH + 1) * k],
+                dst_ref=recvh.at[slot, k],
                 send_sem=s1,
                 recv_sem=r1,
                 device_id={"sub": peer},
                 device_id_type=MESH,
             ).start()
-    recv1[slot] = send1[side, pl.ds(pair, SLAB)]
+    mine_at = SPAN * side + pair
+    recv1[slot] = send1[mine_at + REACH]
+    for k in range(2):
+        recvh[slot, k] = sendh[mine_at + (REACH + 1) * k]
 
     back_at = 4 * (own_block // 2) + 2 * (lane // BLOCK) + lax.rem(own_block, 2)
     p5[...] = dot_ta(jnp.where(back_at == row, 1.0, 0.0).astype(BF16), eye).astype(BF16)
@@ -337,7 +345,7 @@
 
     def seen_flows(weights):
         turned_weights = dot(two_parts(weights), own_map).astype(BF16)
-        sums = dot(turned_weights, recv1[:, REACH].reshape(2 * SUBS, LANES))[:, 0:INTERFACE]
+        sums = dot(turned_weights, recv1[...].reshape(2 * SUBS, LANES))[:, 0:INTERFACE]
         sums = sums[0:BLOCK] + sums[BLOCK : 2 * BLOCK]
         return [sums[RES * j : RES * (j + 1)] for j in range(4)]
 
@@ -356,25 +364,27 @@
         tiles = back_step(tiles)
         weights.append(tiles[REACH])
     weights = jnp.concatenate(weights, axis=0)
-    whole(recv1.at[pl.ds(0, PEERS), REACH], se, re).wait_recv()
-    seen = seen_flows(weights)
     unit = dot_tb(two_parts(weights), own_owners.astype(BF16))
     unit = unit[0:BLOCK] + unit[BLOCK : 2 * BLOCK]
     unit = [unit[RES * j : RES * (j + 1), 0:RES] for j in range(4)]
+    aka[sz] = folded(jnp.concatenate(unit, axis=1))
+    to_z(aka, ska, rka)
+    whole(recv1.at[pl.ds(0, PEERS)], se, re).wait_recv()
+    seen = seen_flows(weights)
     early = draws_of(seen, 3)
     reduce_a(0, early)
-    aka[sz] = folded(jnp.concatenate(unit, axis=1))
-    to_z(aka, ska, rka)
     weights = []
     for _ in range(4):
         tiles = back_step(tiles)
         weights.append(tiles[REACH])
     weights = jnp.concatenate(weights, axis=0)
     seen = seen + seen_flows(weights)
-    reduce_a(1, draws_of(seen, 7))
+    late = seen[7]
+    for j in (6, 5, 4, 3):
+        late = next_power(late, seen, 7, j)
 
     sacc[...] = jnp.zeros((256, LANES), F32)
-    whole(recv1.at[pl.ds(0, PEERS), pl.ds(0, 2 * REACH)], s1, r1).wait_recv()
+    whole(recvh.at[pl.ds(0, PEERS)], s1, r1).wait_recv()
     for k in (2, 1, 3):
         pltpu.make_async_remote_copy(
             src_ref=maps.at[dist],
@@ -386,12 +396,20 @@
         ).start()
     lane_e = iota((PAIR, 128), 1) - (INTERFACE - 128)
     for a in range(SLAB):
-        arrived = recv1[:, a].reshape(2 * SUBS, LANES)
-        part = dot(place_map(a), arrived)
         top = a * PAIR
+        if a == REACH:
+            part = dot(own_map, recv1[...].reshape(2 * SUBS, LANES))
+            low, high = part[:, 0:128], part[:, 128:LANES]
+        else:
+            k, which = (0, a) if a < REACH else (1, a - REACH - 1)
+            low = dot(place_map(a), recvh[:, k, which].reshape(2 * SUBS, 128))
+            high = dot(place_map(a), recvh[:, k, 2].reshape(2 * SUBS, 128))
+            if which:
+                high = pltpu.roll(high, BLOCK, 1)
+            high = jnp.where(lane_e < 0, high, 0.0)
         owner = offs[top : top + PAIR, 4:5].astype(jnp.int32)
         mark = jnp.where((lane_e == owner) & (lane_e >= 0) & (lane_e < RES), 1.0, 0.0)
-        low, high = part[:, 0:128], part[:, 128:LANES] + mark
+        high = high + mark
         zf[top : top + PAIR, 0:128] = low
         zf[top : top + PAIR, 128:LANES] = high
         zb[top : top + PAIR, 0:128] = low.astype(BF16)
@@ -418,9 +436,13 @@
         for i, u in enumerate(us):
             advance(i, u)
 
-    for k in range(6):
+    for j in (2, 1, 0):
+        if j:
+            step()
+        late = next_power(late, seen, 7, j)
+    reduce_a(1, late[:, 0:128])
+    for k in range(4):
         step()
-    reduce_b(0)
     whole(aka.at[pl.ds(0, 7)], ska, rka).wait_recv()
     by_side = [aka[d] + aka[d + 2] + aka[d + 4] + aka[d + 6] for d in range(2)]
     akb[sxy] = jnp.concatenate(by_side, axis=0)
@@ -433,6 +455,7 @@
             device_id={"sub": at + sz},
             device_id_type=MESH,
         ).start()
+    reduce_b(0)
 
     u = half(1)
     prices = (STEP * usum[...]).astype(BF16)
@@ -500,15 +523,6 @@
         return jnp.concatenate(parts, axis=0).astype(BF16)
 
     powers_by = [powers_of(mp.at[d], 4) for d in range(2)]
-    sums = [stack(powers_by[d][1:], in_sum) for d in range(2)]
-    here_sums = jnp.where(side == 0, sums[0], sums[1])
-    there_sums = jnp.where(side == 0, sums[1], sums[0])
-    price_o[side] = STEP * (price0 + dot(marks0.astype(BF16), here_sums))
-    price_copy.wait_recv()
-    sent = price_r[...]
-    price_o[1 - side] = STEP * (
-        sent[:, 0:INTERFACE] + dot(sent[:, INTERFACE:LANES].astype(BF16), there_sums)
-    )
     for d in range(2):
         vfull[d, INTERFACE:LANES] = dot(stack(powers_by[d][0:4], in_price), cts[d]).astype(BF16)
 
@@ -518,13 +532,19 @@
         at = d * BLOCK
         plan_o[d] = -(cs[at : at + BLOCK] + dot(mine[at : at + BLOCK], vfull[d]))
 
-    whole(akc.at[pl.ds(0, 3)], skc, rkc).wait_recv()
+    price_copy.wait_recv()
     whole(maps.at[pl.ds(0, 3)], sc, rc).wait_recv()
-    units, causes = [], []
+    sums = [stack(powers_by[d][1:], in_sum) for d in range(2)]
+    here_sums = jnp.where(side == 0, sums[0], sums[1])
+    there_sums = jnp.where(side == 0, sums[1], sums[0])
+    price_o[side] = STEP * (price0 + dot(marks0.astype(BF16), here_sums))
+    sent = price_r[...]
+    price_o[1 - side] = STEP * (
+        sent[:, 0:INTERFACE] + dot(sent[:, INTERFACE:LANES].astype(BF16), there_sums)
+    )
+    causes = []
     for k in range(DISTS):
-        unit = akc[k]
         for d in range(2):
-            units.append(unfolded(unit[8 * d : 8 * d + 8]))
             size = maps[k, d, 0:1, HORIZON : HORIZON + 1].astype(F32)
             moved = dot2(duals, maps[k, d])
             for j in range(4):
@@ -532,16 +552,18 @@
                 for _ in range(j + 1):
                     part = part * size
                 causes.append(part)
-    units, causes = jnp.concatenate(units, axis=1), two_parts(jnp.concatenate(causes, axis=0))
+    causes = two_parts(jnp.concatenate(causes, axis=0))
+    whole(akc.at[pl.ds(0, 3)], skc, rkc).wait_recv()
+    units = [unfolded(akc[k][8 * d : 8 * d + 8]) for k in range(DISTS) for d in range(2)]
+    units = jnp.concatenate(units, axis=1)
     count = units.shape[1]
     draws1 = dot2(units, causes[0:count]) + dot(units.astype(BF16), causes[count : 2 * count])
     draws1 = draws1[:, 0:HORIZON]
-
     draws0 = reduce_end(1)[:, 0:HORIZON]
     dual_o[...] = duals + (draws0 + draws1 - capacity) * scale
 
     whole(mbuf.at[pl.ds(0, 2 * SLAB - 1)], sm, rm).wait_send()
-    whole(recv1.at[pl.ds(0, PEERS), pl.ds(0, 2 * REACH)], s1, r1).wait_send()
+    whole(recvh.at[pl.ds(0, PEERS)], s1, r1).wait_send()
     whole(recv2.at[pl.ds(0, PEERS)], s2, r2).wait_send()
     for t in range(2):
         all_of(ara, t, 7, sa, ra).wait_send()
@@ -550,7 +572,7 @@
     whole(akb.at[pl.ds(0, 7)], skb, rkb).wait_send()
     whole(akc.at[pl.ds(0, 3)], skc, rkc).wait_send()
     whole(maps.at[pl.ds(0, 3)], sc, rc).wait_send()
-    whole(recv1.at[pl.ds(0, PEERS), REACH], se, re).wait_send()
+    whole(recv1.at[pl.ds(0, PEERS)], se, re).wait_send()
     price_copy.wait_send()
 
 
@@ -591,8 +613,10 @@
             pltpu.VMEM((RES, HORIZON), F32),
             pltpu.VMEM((2, 16, 128), BF16),
             pltpu.VMEM((2, INTERFACE, UNKNOWNS), BF16),
-            pltpu.VMEM((2, PAIRS + 2 * REACH, 2, LANES), BF16),
-            pltpu.VMEM((SUBS, SLAB, 2, LANES), BF16),
+            pltpu.VMEM((2 * SPAN, 2, LANES), BF16),
+            pltpu.VMEM((SUBS, 2, LANES), BF16),
+            pltpu.VMEM((2 * SPAN, 3, 2, 128), BF16),
+            pltpu.VMEM((SUBS, 2, 3, 2, 128), BF16),
             pltpu.VMEM((SUBS, 2, LANES), BF16),
             pltpu.VMEM((SUBS, 2, LANES), BF16),
             pltpu.VMEM((2 * SLAB, 16, 128), BF16),

time: 38 us -> 37.2 us (0.979)
  Pallas kernels: 37.2 us -> 36.5 us
    pallas_call x1, Pallas kernels: 36.4 us -> 35.7 us  [on_device(): pl.pallas_call(kernel, out_shape=(pltpu.VMEM((2, BLOCK, UNKNOWNS), F32),...]
where the time goes in v6:
time: 37.2 us; the launch traced here: 37.1 us
  Pallas kernels  36.5 us (98%)
  between operations  0.64 us (2%)
    pallas_call x1, Pallas kernels, on_device(): pl.pallas_call(kernel, out_shape=(pltpu.VMEM((2, BLOCK, UNKNOWNS), F32),...  35.7 us
    pallas_call x1, Pallas kernels, on_device(): pl.pallas_call(write_out, out_shape=(jax.ShapeDtypeStruct((2, BLOCK, UNKN...  0.82 us

profile of v6, /device:TPU:1, one launch (start us, length us, event | category | flops | bytes accessed | tf_op | source)
XLA Modules:
  0.0 37.1 jit_solution(1732246778351570290)
XLA Ops:
  0.6 35.7 %shard_map.94 = (f32[2,64,768]{2,1,0:T(8,128)S(1)}, f32[2,64,192]{2,1,0:T(8,128)S(1)}, f32[16,48]{1,0:T(8,128)S(1)}) custom-call(bf16[2,64,768]{2,1,0:T(8,128)(2,1)} %cost.1, bf16[2,192,768]{2,1,0:T(8,128)(2,1)} %bitcast.5, bf16[2,768,768]{2,1,0:T(8,128)(2,1)} %solve.1, s32[32,2,128]{2,1,0:T(2,128)} %bitcast.6, s32[2,4,64]{2,1,0:T(4,128)} %bitcast.7, ...), custom_call_target="tpu_custom_call" | custom-call | tf_op jit(solution)/shard_map/pallas_call | solution.py:595
  36.3 0.8 %shard_map.95 = (f32[2,64,768]{2,1,0:T(8,128)}, f32[2,64,192]{2,1,0:T(8,128)}, f32[16,48]{1,0:T(8,128)}) custom-call(f32[2,64,768]{2,1,0:T(8,128)S(1)} %get-tuple-element.6.plan, f32[2,64,192]{2,1,0:T(8,128)S(1)} %get-tuple-element.7.price, f32[16,48]{1,0:T(8,128)S(1)} %get-tuple-element.8.dual), custom_call_target="tpu_custom_call" | custom-call | tf_op jit(solution)/shard_map/pallas_call | solution.py:653

commit v7 on v6

--- a/solution.py
+++ b/solution.py
@@ -72,7 +72,7 @@
     cost, coup, solve, rel_h, near_h, owner_h, cap_h,
     plan_o, price_o, dual_o,
     X, S, C, cs, vfull, rel, near_in, owner_in, cap, meta, cts, send1, recv1, sendh, recvh, send2, recv2,
-    mbuf, offs, L2, lown, p4t, p5, mp, zf, zb, sacc, usum, ara, arb, aka, akb, akc, maps, price_s, price_r,
+    mbuf, offs, L2, lown, p4t, p5, mp, zf, zb, sacc, usum, ara, arb, aka, akb, akc, maps, tops, price_s, price_r,
 
     load_sem, s1, r1, s2, r2, sm, rm, sp, rp, sa, ra, sb, rb, ska, rka, skb, rkb, sc, rc, se, re, skc, rkc,
 ):
@@ -234,6 +234,10 @@
         for j in range(4):
             if j:
                 small_map = dot2(small_map, wide_map) / size
+            padded = jnp.concatenate(
+                [small_map, jnp.zeros((HORIZON, LANES - INTERFACE), F32)], axis=1
+            )
+            tops[d, :, LANES * j : LANES * (j + 1)] = two_parts(padded)
             tiles += [small_map[:, 0:HORIZON], jnp.broadcast_to(size, (HORIZON, BLOCK - HORIZON))]
         maps[dist, d] = jnp.concatenate(tiles, axis=1).astype(BF16)
 
@@ -512,25 +516,26 @@
     in_price = (1.0, -0.9, 0.27, -0.027)
     in_sum = (-4.0, 1.8, -0.36, 0.027)
 
-    def powers_of(m_ref, count):
+    def powers_of(d):
+        moved = dot2(duals, tops[d, 0:HORIZON]) + dot(
+            duals.astype(BF16), tops[d, HORIZON : 2 * HORIZON]
+        )
+        size = maps[dist, d, 0:1, HORIZON : HORIZON + 1].astype(F32)
         powers = [wide]
-        for _ in range(count):
-            powers.append(dot2(powers[-1], m_ref[0:INTERFACE, 0:INTERFACE]) * (-1.0 / STEP))
+        for j in range(4):
+            part = moved[:, LANES * j : LANES * j + INTERFACE]
+            for _ in range(j + 1):
+                part = part * size * (-1.0 / STEP)
+            powers.append(part)
         return powers
 
     def stack(powers, weights):
         parts = [p * (w / b) for p, w, b in zip(powers, weights, binom)]
         return jnp.concatenate(parts, axis=0).astype(BF16)
 
-    powers_by = [powers_of(mp.at[d], 4) for d in range(2)]
+    powers_by = [powers_of(d) for d in range(2)]
     for d in range(2):
         vfull[d, INTERFACE:LANES] = dot(stack(powers_by[d][0:4], in_price), cts[d]).astype(BF16)
-
-    whole(recv2.at[pl.ds(0, PEERS)], s2, r2).wait_recv()
-    mine = dot(p5[...], recv2[...].reshape(2 * SUBS, LANES)).astype(BF16)
-    for d in range(2):
-        at = d * BLOCK
-        plan_o[d] = -(cs[at : at + BLOCK] + dot(mine[at : at + BLOCK], vfull[d]))
 
     price_copy.wait_recv()
     whole(maps.at[pl.ds(0, 3)], sc, rc).wait_recv()
@@ -553,6 +558,12 @@
                     part = part * size
                 causes.append(part)
     causes = two_parts(jnp.concatenate(causes, axis=0))
+    whole(recv2.at[pl.ds(0, PEERS)], s2, r2).wait_recv()
+    mine = dot(p5[...], recv2[...].reshape(2 * SUBS, LANES)).astype(BF16)
+    for d in range(2):
+        at = d * BLOCK
+        plan_o[d] = -(cs[at : at + BLOCK] + dot(mine[at : at + BLOCK], vfull[d]))
+
     whole(akc.at[pl.ds(0, 3)], skc, rkc).wait_recv()
     units = [unfolded(akc[k][8 * d : 8 * d + 8]) for k in range(DISTS) for d in range(2)]
     units = jnp.concatenate(units, axis=1)
@@ -636,6 +647,7 @@
             pltpu.VMEM((8, 16, 128), F32),
             pltpu.VMEM((DISTS, 16, 128), F32),
             pltpu.VMEM((DISTS, 2, HORIZON, LANES), BF16),
+            pltpu.VMEM((2, 2 * HORIZON, 4 * LANES), BF16),
             pltpu.VMEM((BLOCK, LANES), F32),
             pltpu.VMEM((BLOCK, LANES), F32),
             dma((10,)),

time: 37.2 us -> 37.2 us (level)
  no operation moved by 1% of the time
where the time goes in v7:
time: 37.2 us; the launch traced here: 37.1 us
  Pallas kernels  36.4 us (98%)
  between operations  0.64 us (2%)
    pallas_call x1, Pallas kernels, on_device(): pl.pallas_call(kernel, out_shape=(pltpu.VMEM((2, BLOCK, UNKNOWNS), F32),...  35.6 us
    pallas_call x1, Pallas kernels, on_device(): pl.pallas_call(write_out, out_shape=(jax.ShapeDtypeStruct((2, BLOCK, UNKN...  0.82 us

profile of v7, /device:TPU:1, one launch (start us, length us, event | category | flops | bytes accessed | tf_op | source)
XLA Modules:
  0.0 37.1 jit_solution(18348264429844303418)
XLA Ops:
  0.6 35.6 %shard_map.94 = (f32[2,64,768]{2,1,0:T(8,128)S(1)}, f32[2,64,192]{2,1,0:T(8,128)S(1)}, f32[16,48]{1,0:T(8,128)S(1)}) custom-call(bf16[2,64,768]{2,1,0:T(8,128)(2,1)} %cost.1, bf16[2,192,768]{2,1,0:T(8,128)(2,1)} %bitcast.5, bf16[2,768,768]{2,1,0:T(8,128)(2,1)} %solve.1, s32[32,2,128]{2,1,0:T(2,128)} %bitcast.6, s32[2,4,64]{2,1,0:T(4,128)} %bitcast.7, ...), custom_call_target="tpu_custom_call" | custom-call | tf_op jit(solution)/shard_map/pallas_call | solution.py:606
  36.3 0.8 %shard_map.95 = (f32[2,64,768]{2,1,0:T(8,128)}, f32[2,64,192]{2,1,0:T(8,128)}, f32[16,48]{1,0:T(8,128)}) custom-call(f32[2,64,768]{2,1,0:T(8,128)S(1)} %get-tuple-element.6.plan, f32[2,64,192]{2,1,0:T(8,128)S(1)} %get-tuple-element.7.price, f32[16,48]{1,0:T(8,128)S(1)} %get-tuple-element.8.dual), custom_call_target="tpu_custom_call" | custom-call | tf_op jit(solution)/shard_map/pallas_call | solution.py:665
